TPU v7x, 8 devices: a whole 2x2x1 slice. The times are simulated.
8 devices in a mesh: dp: 2 (over z, y), tp: 4 (over x, core).
Axes of the slice: x: 2, y: 2, z: 1, core: 2. Of those that a mesh axis runs over, the one named last changes fastest.
Arguments:
- x_in: bfloat16 [2, 64, 3072], P('dp', 'tp'), parts along dimension 0
- start_pos: int32 [2], P('dp'), parts along dimension 0
- k_cache: bfloat16 [2, 4096, 8, 128], P('dp', None, 'tp'), parts along dimension 0
- v_cache: bfloat16 [2, 4096, 8, 128], P('dp', None, 'tp'), parts along dimension 0
- attn_gain: bfloat16 [3072], replicated
- w_query: bfloat16 [3072, 24, 128], P(None, 'tp')
- w_key: bfloat16 [3072, 8, 128], P(None, 'tp')
- w_value: bfloat16 [3072, 8, 128], P(None, 'tp')
- w_out: bfloat16 [24, 128, 3072], P('tp')
- mlp_gain: bfloat16 [3072], replicated
- w_gate: bfloat16 [3072, 8192], P(None, 'tp')
- w_up: bfloat16 [3072, 8192], P(None, 'tp')
- w_down: bfloat16 [8192, 3072], P('tp')
Outputs:
- output 1: bfloat16 [2, 64, 3072], P('dp', 'tp'), parts along dimension 0
- output 2: bfloat16 [2, 4096, 8, 128], P('dp', None, 'tp'), parts along dimension 0
- output 3: bfloat16 [2, 4096, 8, 128], P('dp', None, 'tp'), parts along dimension 0
There are 2 independent parts. A program takes and returns all parts, laid end to end along the dimension named above; an argument that names none is the same for every part.
All inputs are finite; a program needn't handle non-finite values.
Results may differ from a plain program's by a relative error of at most 0.0131868.
Values are sent between devices in bfloat16 or wider.
A program may use at most 1 GiB of HBM per device.

v0:
```python
import jax
import jax.numpy as jnp
from jax import lax
from jax.sharding import PartitionSpec as P

ROPE_BASE = 10000.0
NORM_EPS = 1e-5


def rms_norm(rows, gain):
    rows32 = rows.astype(jnp.float32)
    inv_rms = lax.rsqrt(jnp.mean(rows32 * rows32, axis=-1, keepdims=True) + NORM_EPS)
    return (rows32 * inv_rms * gain.astype(jnp.float32)).astype(jnp.bfloat16)


def rotate(heads_in, positions):
    head_dim = heads_in.shape[-1]
    inv_freq = jnp.power(ROPE_BASE, -jnp.arange(0, head_dim, 2).astype(jnp.float32) / head_dim)
    angles = positions.astype(jnp.float32)[..., None] * inv_freq
    lead = angles.shape[:2] + (1,) * (heads_in.ndim - 3) + (head_dim // 2,)
    cos_t = jnp.cos(angles).reshape(lead)
    sin_t = jnp.sin(angles).reshape(lead)
    pairs = heads_in.reshape(heads_in.shape[:-1] + (head_dim // 2, 2))
    even = pairs[..., 0]
    odd = pairs[..., 1]
    turned = jnp.stack([even * cos_t - odd * sin_t, even * sin_t + odd * cos_t], axis=-1)
    return turned.reshape(heads_in.shape)


def project_qkv(normed, positions, w_query, w_key, w_value):
    model_dim, kv_loc, head_dim = w_key.shape
    group = w_query.shape[1] // kv_loc
    w_query4 = w_query.reshape(model_dim, kv_loc, group, head_dim)
    q_lin = jnp.einsum('btd,dkge->btkge', normed, w_query4, preferred_element_type=jnp.float32)
    k_lin = jnp.einsum('btd,dke->btke', normed, w_key, preferred_element_type=jnp.float32)
    v_chunk = jnp.einsum('btd,dke->btke', normed, w_value, preferred_element_type=jnp.float32).astype(jnp.bfloat16)
    queries = rotate(q_lin, positions).astype(jnp.bfloat16)
    k_chunk = rotate(k_lin, positions).astype(jnp.bfloat16)
    return queries, k_chunk, v_chunk


def attend(queries, k_chunk, v_chunk, k_cache, v_cache, start_pos, tile_rows):
    rows, chunk_len, kv_loc, group, head_dim = queries.shape
    window = k_cache.shape[1]
    q_block = chunk_len
    while q_block > 8 and tile_rows * q_block > 256:
        q_block = q_block // 2
    n_blocks = chunk_len // q_block
    scale = head_dim ** -0.5
    offsets = jnp.mod(jnp.arange(window)[None, :] - start_pos[:, None], window)
    cache_valid = (start_pos[:, None] - window + offsets) >= 0
    key_ids = jnp.arange(chunk_len)

    def one_block(block):
        first = block * q_block
        q_tile = lax.dynamic_slice_in_dim(queries, first, q_block, axis=1)
        q_ids = first + jnp.arange(q_block)
        cache_mask = cache_valid[:, None, :] & (offsets[:, None, :] > q_ids[None, :, None])
        chunk_mask = key_ids[None, :] <= q_ids[:, None]
        s_cache = jnp.einsum('bqkge,bske->bkgqs', q_tile, k_cache, preferred_element_type=jnp.float32) * scale
        s_chunk = jnp.einsum('bqkge,bske->bkgqs', q_tile, k_chunk, preferred_element_type=jnp.float32) * scale
        s_cache = jnp.where(cache_mask[:, None, None], s_cache, -jnp.inf)
        s_chunk = jnp.where(chunk_mask, s_chunk, -jnp.inf)
        top = jnp.maximum(jnp.max(s_cache, axis=-1, keepdims=True), jnp.max(s_chunk, axis=-1, keepdims=True))
        e_cache = jnp.exp(s_cache - top)
        e_chunk = jnp.exp(s_chunk - top)
        total_mass = jnp.sum(e_cache, axis=-1, keepdims=True) + jnp.sum(e_chunk, axis=-1, keepdims=True)
        p_cache = (e_cache / total_mass).astype(jnp.bfloat16)
        p_chunk = (e_chunk / total_mass).astype(jnp.bfloat16)
        mixed = jnp.einsum('bkgqs,bske->bqkge', p_cache, v_cache, preferred_element_type=jnp.float32)
        mixed = mixed + jnp.einsum('bkgqs,bske->bqkge', p_chunk, v_chunk, preferred_element_type=jnp.float32)
        return mixed.astype(jnp.bfloat16)

    tiles = lax.map(one_block, jnp.arange(n_blocks))
    return tiles.reshape(n_blocks, rows, q_block, kv_loc * group, head_dim)


def write_chunk(cache, chunk, start_pos):
    window = cache.shape[1]
    chunk_len = chunk.shape[1]

    def one_row(old_rows, new_rows, start):
        filler = jnp.zeros((window - chunk_len,) + new_rows.shape[1:], new_rows.dtype)
        doubled = jnp.concatenate([new_rows, filler, new_rows, filler], axis=0)
        shift = jnp.mod(start, window)
        placed = lax.dynamic_slice_in_dim(doubled, window - shift, window, axis=0)
        offsets = jnp.mod(jnp.arange(window) - start, window)
        return jnp.where((offsets < chunk_len)[:, None, None], placed, old_rows)

    return jax.vmap(one_row)(cache, chunk, start_pos)


def swiglu(mlp_rows, w_gate, w_up):
    gate = jnp.einsum('btd,df->btf', mlp_rows, w_gate, preferred_element_type=jnp.float32)
    up_proj = jnp.einsum('btd,df->btf', mlp_rows, w_up, preferred_element_type=jnp.float32)
    return (jax.nn.silu(gate) * up_proj).astype(jnp.bfloat16)


def solution(mesh):
    row_spec = P('dp', 'tp', None)
    cache_spec = P('dp', None, 'tp', None)
    head_cols = P(None, 'tp', None)
    in_specs = (row_spec, P('dp'), cache_spec, cache_spec, P(), head_cols, head_cols, head_cols, P('tp', None, None), P(), P(None, 'tp'), P(None, 'tp'), P('tp', None))
    out_specs = (row_spec, cache_spec, cache_spec)

    def local_layer(x_in, start_pos, k_cache, v_cache, attn_gain, w_query, w_key, w_value, w_out, mlp_gain, w_gate, w_up, w_down):
        rows = x_in.shape[0]
        model_dim = x_in.shape[2]
        attn_rows = lax.all_gather(rms_norm(x_in, attn_gain), 'tp', axis=1, tiled=True)
        chunk_len = attn_rows.shape[1]
        positions = start_pos[:, None] + jnp.arange(chunk_len)[None, :]
        queries, k_chunk, v_chunk = project_qkv(attn_rows, positions, w_query, w_key, w_value)
        mixed = attend(queries, k_chunk, v_chunk, k_cache, v_cache, start_pos, rows)
        attn_part = jnp.einsum('nbqhe,hed->bnqd', mixed, w_out, preferred_element_type=jnp.float32)
        attn_part = attn_part.reshape(rows, chunk_len, model_dim).astype(jnp.bfloat16)
        attn_sum = lax.psum_scatter(attn_part, 'tp', scatter_dimension=1, tiled=True)
        hidden = (x_in.astype(jnp.float32) + attn_sum.astype(jnp.float32)).astype(jnp.bfloat16)
        mlp_rows = lax.all_gather(rms_norm(hidden, mlp_gain), 'tp', axis=1, tiled=True)
        activated = swiglu(mlp_rows, w_gate, w_up)
        mlp_part = jnp.einsum('btf,fd->btd', activated, w_down, preferred_element_type=jnp.float32).astype(jnp.bfloat16)
        mlp_sum = lax.psum_scatter(mlp_part, 'tp', scatter_dimension=1, tiled=True)
        x_out = (hidden.astype(jnp.float32) + mlp_sum.astype(jnp.float32)).astype(jnp.bfloat16)
        return x_out, write_chunk(k_cache, k_chunk, start_pos), write_chunk(v_cache, v_chunk, start_pos)

    return jax.shard_map(local_layer, mesh=mesh, in_specs=in_specs, out_specs=out_specs, check_vma=False)
```

profile of v0, /device:TPU:0, one launch (start us, length us, event | category | flops | bytes accessed | tf_op | source)
XLA Modules:
  0.0 162.1 jit_solution(1216567387865058319)
XLA Ops:
  8.0 0.7 convert_element_type.134
  8.7 1.0 fusion.50
  9.8 1.0 fusion.52
  10.7 11.3 %all_gather.6 = bf16[1,64,3072]{2,1,0:T(8,128)(2,1)} all-gather(bf16[1,16,3072]{2,1,0:T(8,128)(2,1)S(1)} %fusion.52), channel_id=1, replica_groups=mesh['dp'=2,'tp'=4] {'tp'}, dimensions={1}, use_global_device_ids=true | all-gather | bytes 491520 | tf_op jit(solution)/shard_map/all_gather | solution.py:109
  22.1 12.6 %copy.23 = bf16[3072,2,3,128]{0,1,3,2:T(2,128)(2,1)} copy(bf16[3072,2,3,128]{3,0,2,1:T(8,128)(2,1)} %bitcast.111) | data formatting | bytes 9437184 | tf_op jit(solution)/shard_map/reshape | solution.py:33
  34.9 5.6 %fusion.19 = f32[1,64,2,3,64,2]{4,1,5,3,2,0:T(8,128)S(1)} fusion(bf16[2,3,64,2,3072]{4,0,3,2,1:T(2,128)(2,1)} %bitcast.112, bf16[1,64,3072]{2,1,0:T(8,128)(2,1)} %all_gather.6), kind=kOutput, calls=%fused_computation.33 | convolution fusion | flops 301989888 | bytes 5308416 | tf_op jit(solution)/shard_map/btd,dkge->btkge/dot_general | solution.py:34
  40.8 3.7 %copy.28 = bf16[2,128,3072]{2,0,1:T(2,128)(2,1)} copy(bf16[2,128,3072]{1,0,2:T(2,128)(2,1)S(1)} %bitcast.116) | data formatting | bytes 3145728 | tf_op jit(solution)/shard_map/btd,dke->btke/dot_general | solution.py:35
  44.5 2.4 %fusion.29 = f32[1,64,2,64,2]{3,1,4,2,0:T(8,128)S(1)} fusion(bf16[2,64,2,3072]{3,0,2,1:T(2,128)(2,1)} %bitcast.117, bf16[1,64,3072]{2,1,0:T(8,128)(2,1)} %all_gather.6), kind=kOutput, calls=%fused_computation.39 | convolution fusion | flops 100663296 | bytes 2031616 | tf_op jit(solution)/shard_map/btd,dke->btke/dot_general | solution.py:35
  47.3 0.2 fusion.68
  47.6 3.2 %fusion.67 = (f32[2,3,64]{2,1,0:T(4,128)S(1)}, f32[1,2,3,64,4096]{4,3,2,1,0:T(8,128)S(1)}) fusion(bf16[64,2,3,128]{0,3,2,1:T(8,128)(2,1)S(1)} %bitcast.115, bf16[4096,2,128,1]{2,1,0,3:T(2,128)(2,1)} %bitcast.110, pred[64,4096]{1,0:T(8,128)(4,1)S(1)} %fusion.36), kind=kOutput, calls=%fused_computation.99 | convolution fusion | flops 407371392 | bytes 8750592 | tf_op jit(solution)/shard_map/while/body/eval_jaxpr/bqkge,bske->bkgqs/dot_general | solution.py:60
  50.9 1.0 fusion
  51.9 0.4 fusion.33
  52.6 1.8 %fusion.23 = f32[2,128,3,64]{1,3,2,0:T(8,128)S(1)} fusion(bf16[4096,2,128,1]{2,1,0,3:T(2,128)(2,1)S(1)} %bitcast.113, f32[2,3,64]{2,1,0:T(4,128)S(1)} %add.154, f32[1,2,3,64,4096]{4,3,2,1,0:T(8,128)S(1)} %get-tuple-element.64, f32[2,3,64]{2,1,0:T(4,128)S(1)} %max.9), kind=kOutput, calls=%fused_computation.37 | convolution fusion | flops 407371776 | bytes 8588288 | tf_op jit(solution)/shard_map/while/body/eval_jaxpr/bkgqs,bske->bqkge/dot_general | solution.py:70
  54.4 0.2 fusion.28
  54.7 1.7 %fusion.4 = bf16[1,64,3072]{2,1,0:T(8,128)(2,1)} fusion(bf16[64,6,128]{2,0,1:T(8,128)(2,1)S(1)} %bitcast.120, bf16[6,128,3072]{2,1,0:T(8,128)(2,1)S(1)} %bitcast.109), kind=kOutput, calls=%fused_computation.17 | convolution fusion | flops 302186496 | bytes 5210112 | tf_op jit(solution)/shard_map/nbqhe,hed->bnqd/dot_general | solution.py:114
  56.7 15.2 %reduce-scatter.3.cloned.1.call-done = bf16[1,16,3072]{2,1,0:T(8,128)(2,1)} async-done(((bf16[1,64,3072]{2,1,0:T(8,128)(2,1)}), bf16[1,16,3072]{2,1,0:T(8,128)(2,1)}) %reduce-scatter.3.cloned.1.call-update) | async-done | bytes 98320 | tf_op jit(solution)/shard_map/reduce_scatter | solution.py:116
  71.9 1.0 fusion.54
  72.9 1.0 fusion.56
  73.9 8.5 %all_gather.7 = bf16[1,64,3072]{2,1,0:T(8,128)(2,1)S(1)} all-gather(bf16[1,16,3072]{2,1,0:T(8,128)(2,1)S(1)} %fusion.56), channel_id=1, replica_groups=mesh['dp'=2,'tp'=4] {'tp'}, dimensions={1}, use_global_device_ids=true | all-gather | bytes 491520 | tf_op jit(solution)/shard_map/all_gather | solution.py:118
  82.5 6.9 %fusion.46 = f32[64,2048]{1,0:T(8,128)S(1)} fusion(bf16[3072,2048]{1,0:T(8,128)(2,1)} %param.23, bf16[1,64,3072]{2,1,0:T(8,128)(2,1)S(1)} %all_gather.7), kind=kOutput, calls=%fused_computation.52 | convolution fusion | flops 805306368 | bytes 13500416 | tf_op jit(solution)/shard_map/btd,df->btf/dot_general | solution.py:94
  89.3 13.4 %fusion.5 = bf16[1,64,3072]{2,1,0:T(8,128)(2,1)} fusion(bf16[2048,3072]{1,0:T(8,128)(2,1)} %param.25, bf16[3072,2048]{1,0:T(8,128)(2,1)} %param.24, f32[64,2048]{1,0:T(8,128)S(1)} %fusion.46, bf16[1,64,3072]{2,1,0:T(8,128)(2,1)S(1)} %all_gather.7), kind=kOutput, calls=%fused_computation.18 | convolution fusion | flops 1611595776 | bytes 26476544 | tf_op jit(solution)/shard_map/btf,fd->btd/dot_general | solution.py:120
  102.8 1.1 broadcast.374
  103.9 49.8 %broadcast_select_fusion = (bf16[1,4096,2,128]{3,2,1,0:T(2,128)(2,1)}, bf16[1,4096,2,128]{3,2,1,0:T(2,128)(2,1)}) fusion(bf16[1,4096,2,128]{3,2,1,0:T(2,128)(2,1)} %param.16, pred[4096]{0:T(1024)(128)(4,1)S(1)} %get-tuple-element.68, s32[]{:T(128)} %bitcast.43, bf16[1,64,2,128]{3,2,1,0:T(2,128)(2,1)S(1)} %copy.39, ...), kind=kLoop, calls=%fused_computation.12 | loop fusion | flops 8388608 | bytes 10522628 | tf_op jit(solution)/shard_map/vmap(jit(_where))/select_n | solution.py:88
  153.7 1.6 fusion.57
  (55 shorter events, 1.5 us)
Async XLA Ops:
  7.2 44.7 %copy-start = (bf16[3072,2,128]{2,1,0:T(2,128)(2,1)S(1)}, bf16[3072,2,128]{2,1,0:T(2,128)(2,1)}, u32[]{:S(2)}) copy-start(bf16[3072,2,128]{2,1,0:T(2,128)(2,1)} %param.20) | copy-start | bytes 4718596
  7.2 64.7 %reduce-scatter.3.cloned.1.call-start = ((), (), s32[]{:S(2)}) async-start(), calls=%async_computation.2 | async-start | bytes 491520 | tf_op jit(solution)/shard_map/reduce_scatter | solution.py:116
  34.9 5.7 %copy-start.7 = (f32[64,64]{1,0:T(8,128)}, f32[64,64]{1,0:T(8,128)S(1)}, u32[]{:S(2)}) copy-start(f32[64,64]{1,0:T(8,128)S(1)} %get-tuple-element.61) | copy-start | bytes 49156
  34.9 5.7 %copy-start.9 = (f32[64,64]{1,0:T(8,128)}, f32[64,64]{1,0:T(8,128)S(1)}, u32[]{:S(2)}) copy-start(f32[64,64]{1,0:T(8,128)S(1)} %get-tuple-element.62) | copy-start | bytes 49156
  34.9 5.9 %copy-start.4 = (bf16[3072,2,128]{2,1,0:T(2,128)(2,1)S(1)}, bf16[3072,2,128]{2,1,0:T(2,128)(2,1)}, u32[]{:S(2)}) copy-start(bf16[3072,2,128]{2,1,0:T(2,128)(2,1)} %param.19) | copy-start | bytes 4718596
  40.8 6.1 %copy-start.8 = (f32[64,64]{1,0:T(8,128)S(1)}, f32[64,64]{1,0:T(8,128)}, u32[]{:S(2)}) copy-start(f32[64,64]{1,0:T(8,128)} %copy-done.7) | copy-start | bytes 49156
  40.8 6.1 %copy-start.10 = (f32[64,64]{1,0:T(8,128)S(1)}, f32[64,64]{1,0:T(8,128)}, u32[]{:S(2)}) copy-start(f32[64,64]{1,0:T(8,128)} %copy-done.9) | copy-start | bytes 49156
  50.8 1.1 copy-start.6
  50.9 1.7 %copy-start.3 = (bf16[1,4096,2,128]{3,2,1,0:T(2,128)(2,1)S(1)}, bf16[1,4096,2,128]{3,2,1,0:T(2,128)(2,1)}, u32[]{:S(2)}) copy-start(bf16[1,4096,2,128]{3,2,1,0:T(2,128)(2,1)} %param.16) | copy-start | bytes 6291460
  51.9 2.8 %slice-start = ((s8[4718592]{0:T(1024)(128)(4,1)}), s8[4194304]{0:T(1024)(128)(4,1)S(1)}, s32[]{:S(2)}) async-start(s8[4718592]{0:T(1024)(128)(4,1)} %bitcast.108), calls=%async_computation.4 | async-start | bytes 8388608
  52.6 2.1 %slice-start.1 = ((s8[4718592]{0:T(1024)(128)(4,1)}), s8[524288]{0:T(1024)(128)(4,1)S(1)}, s32[]{:S(2)}) async-start(s8[4718592]{0:T(1024)(128)(4,1)} %bitcast.108), calls=%async_computation.5 | async-start | bytes 1048576
  54.7 1.8 %copy-start.11 = (bf16[3072]{0:T(1024)(128)(2,1)S(1)}, bf16[3072]{0:T(1024)(128)(2,1)}, u32[]{:S(2)}) copy-start(bf16[3072]{0:T(1024)(128)(2,1)} %param.22) | copy-start | bytes 18436
  54.7 17.2 %copy-start.2 = (bf16[1,16,3072]{2,1,0:T(8,128)(2,1)S(1)}, bf16[1,16,3072]{2,1,0:T(8,128)(2,1)}, u32[]{:S(2)}) copy-start(bf16[1,16,3072]{2,1,0:T(8,128)(2,1)} %param.13) | copy-start | bytes 294916
  56.4 97.3 %reduce-scatter.5.cloned.1.call-start = ((), (), s32[]{:S(2)}) async-start(), calls=%async_computation.3 | async-start | bytes 491520 | tf_op jit(solution)/shard_map/reduce_scatter | solution.py:121
  102.8 52.5 %copy-start.1 = (bf16[3072,2,128]{2,1,0:T(2,128)(2,1)S(1)}, bf16[3072,2,128]{2,1,0:T(2,128)(2,1)}, u32[]{:S(2)}) copy-start(bf16[3072,2,128]{2,1,0:T(2,128)(2,1)} %param.20) | copy-start | bytes 4718596
  103.9 49.8 %copy-start.5 = (bf16[1,16,3072]{2,1,0:T(8,128)(2,1)S(1)}, bf16[1,16,3072]{2,1,0:T(8,128)(2,1)}, u32[]{:S(2)}) copy-start(bf16[1,16,3072]{2,1,0:T(8,128)(2,1)} %reduce-scatter.3.cloned.1.call-done) | copy-start | bytes 294916
Sparse Core Ops, SparseCore 0:
  56.6 15.2 reduce-scatter.2
  102.9 16.2 reduce-scatter.4
where the time goes:
time: 163 us; the launch traced here: 162 us
  other arithmetic  57.7 us (35%)
  matrix products  35.9 us (22%)
  blocking collectives  19.9 us (12%)
  local copies, waits for them, and re-layouts  18.1 us (11%)
  waiting for transfers between devices  15.2 us (9%)
  between operations  15.2 us (9%)
    select_n x1, other arithmetic, one_row(): return jnp.where((offsets < chunk_len)[:, None, None], placed, old_rows)  49.8 us
    reduce_scatter x1, waiting for transfers between devices, local_layer(): lax.psum_scatter(attn_part, 'tp', scatter_dimension=1, tiled=True)  15.2 us
    dot_general x1, matrix products, local_layer(): jnp.einsum('btf,fd->btd', activated, w_down, preferred_element_type=jnp.f...  13.4 us
    reshape x1, local copies, waits for them, and re-layouts, project_qkv(): w_query4 = w_query.reshape(model_dim, kv_loc, group, head_dim)  12.6 us
    all_gather x1, blocking collectives, local_layer(): lax.all_gather(rms_norm(x_in, attn_gain), 'tp', axis=1, tiled=True)  11.3 us
    all_gather x1, blocking collectives, local_layer(): lax.all_gather(rms_norm(hidden, mlp_gain), 'tp', axis=1, tiled=True)  8.53 us
    dot_general x1, matrix products, swiglu(): jnp.einsum('btd,df->btf', mlp_rows, w_gate, preferred_element_type=jnp.fl...  6.87 us
    dot_general x1, matrix products, project_qkv(): jnp.einsum('btd,dkge->btkge', normed, w_query4, preferred_element_type=jn...  5.56 us
  transfers between devices with their start and end apart: 2, of which 1 were waited for; matrix products, arithmetic and copies ran while one was open for 31% of the time, Pallas kernels for 0%

commit v1 on v0

v1 whole, which is shorter than its diff:
```python
import functools

import jax
import jax.numpy as jnp
import numpy as np
from jax import lax
from jax.experimental import pallas as pl
from jax.experimental.pallas import tpu as pltpu
from jax.sharding import PartitionSpec as P

ROPE_BASE = 10000.0
NORM_EPS = 1e-5
MESH = pl.DeviceIdType.MESH
BF16 = jnp.bfloat16
F32 = jnp.float32
HD = 128
NCH = 4
KB = 512


def dot(a, b):
    return jnp.dot(a, b, preferred_element_type=F32)


def dot_t(a, b):
    return lax.dot_general(a, b, (((1,), (1,)), ((), ())), preferred_element_type=F32)


def layer_kernel(start_ref, invf_ref, x_hbm, g1_hbm, g2_hbm, kc_hbm, vc_hbm, wq_hbm, wk_hbm, wv_hbm, wo_hbm, wg_hbm, wu_hbm, wd_hbm,
                 xo_hbm, kn_hbm, vn_hbm,
                 xall, nbuf, g1, g2, kbuf, vbuf, wq, wk, wv, wo, wg, wu, wd,
                 sbuf, qbuf, kch, vch, obuf, part, rx1, cs, rx2, hbuf, ubuf, part2, rx4, cs2, rx5, xout, kout, vout,
                 ld_sem, st_sem, ag_send, ag_recv, s1, r1, s2, r2, s3, r3, s4, r4, s5, r5):
    T = xall.shape[0]
    D = xall.shape[1]
    CW = D // NCH
    HW = CW // 2
    tb = T // 4
    window = kbuf.shape[0] * 128
    me = lax.axis_index('tp')
    core = lax.rem(me, 2)
    chip = lax.div(me, 2)
    partner = chip * 2 + (1 - core)
    across = (1 - chip) * 2 + core

    def load(i, src, dst):
        return pltpu.make_async_copy(src, dst, ld_sem.at[i])

    def rows_of(owner):
        return pl.ds(pl.multiple_of(owner * tb, tb), tb)

    def remote(src, dst, send, recv, dev):
        return pltpu.make_async_remote_copy(src_ref=src, dst_ref=dst, send_sem=send, recv_sem=recv, device_id={'tp': dev}, device_id_type=MESH)

    barrier = pltpu.get_barrier_semaphore()
    for other in (partner, across):
        pl.semaphore_signal(barrier, inc=1, device_id={'tp': other}, device_id_type=MESH)

    own = xall.at[rows_of(me)]
    loads = [load(0, x_hbm, own), load(1, g1_hbm, g1), load(2, g2_hbm, g2), load(3, kc_hbm, kbuf), load(4, vc_hbm, vbuf),
             load(5, wk_hbm, wk), load(6, wv_hbm, wv), load(7, wq_hbm, wq), load(8, wo_hbm, wo), load(9, wg_hbm, wg),
             load(10, wu_hbm, wu), load(11, wd_hbm, wd)]
    for item in loads:
        item.start()
    pl.semaphore_wait(barrier, 2)

    loads[0].wait()
    to_partner = remote(own, own, ag_send.at[0], ag_recv.at[0], partner)
    to_across = remote(own, own, ag_send.at[1], ag_recv.at[1], across)
    to_across.start()
    to_partner.start()

    row = lax.broadcasted_iota(jnp.int32, (256, 256), 0)
    col = lax.broadcasted_iota(jnp.int32, (256, 256), 1)
    pick = jnp.where(col == 2 * lax.rem(row, 128) + lax.div(row, 128), 1.0, 0.0).astype(BF16)

    def split(a_ref, b_ref):
        def body(b, carry):
            both = jnp.concatenate([a_ref[b], b_ref[b]], axis=1)
            sep = dot(pick, both).astype(BF16)
            a_ref[b] = sep[:, :128]
            b_ref[b] = sep[:, 128:]
            return carry
        lax.fori_loop(0, a_ref.shape[0], body, 0, unroll=4)

    loads[3].wait()
    loads[4].wait()
    split(kbuf, vbuf)
    loads[5].wait()
    loads[6].wait()
    split(wk, wv)

    start = start_ref[0]
    lane = lax.broadcasted_iota(jnp.int32, (T, HD), 1)
    tok = lax.broadcasted_iota(jnp.int32, (T, HD), 0)
    angles = (start + tok).astype(F32) * invf_ref[...]
    cos_t = jnp.cos(angles)
    even = lax.rem(lane, 2) == 0
    sin_t = jnp.where(even, -jnp.sin(angles), jnp.sin(angles))

    def rope(h):
        swapped = jnp.where(even, pltpu.roll(h, HD - 1, 1), pltpu.roll(h, 1, 1))
        return h * cos_t + swapped * sin_t

    to_across.wait_recv()
    relay = xall.at[rows_of(across)]
    fwd = remote(relay, relay, ag_send.at[2], ag_recv.at[2], partner)
    fwd.start()
    to_partner.wait_recv()
    fwd.wait_recv()

    loads[1].wait()
    loads[2].wait()
    x32 = xall[...].astype(F32)
    inv = lax.rsqrt(jnp.mean(x32 * x32, axis=-1, keepdims=True) + NORM_EPS)
    nbuf[...] = (x32 * inv * g1[...].astype(F32)).astype(BF16)

    loads[7].wait()
    normed = nbuf[...]

    def split_rows(ref, g):
        return ref[:, g * 128:(g + 1) * 128, :].reshape(D, HD)

    k_lin = dot(normed, jnp.concatenate([split_rows(wk, 0), split_rows(wk, 1)], axis=1))
    v_lin = dot(normed, jnp.concatenate([split_rows(wv, 0), split_rows(wv, 1)], axis=1))
    kch[...] = jnp.zeros_like(kch)
    vch[...] = jnp.zeros_like(vch)
    for g in range(2):
        kch[g, :T] = rope(k_lin[:, g * HD:(g + 1) * HD]).astype(BF16)
        vch[g, :T] = v_lin[:, g * HD:(g + 1) * HD].astype(BF16)
    for pair in range(3):
        q_lin = dot(normed, jnp.concatenate([wq[2 * pair], wq[2 * pair + 1]], axis=1))
        for i in range(2):
            head = 2 * pair + i
            qbuf[head // 3, (head % 3) * T:(head % 3 + 1) * T] = rope(q_lin[:, i * HD:(i + 1) * HD]).astype(BF16)

    prow = lax.broadcasted_iota(jnp.int32, (2 * T, HD), 0)
    pcol = lax.broadcasted_iota(jnp.int32, (2 * T, HD), 1)
    for src, dst in ((kch, kout), (vch, vout)):
        mix = sum(dot(jnp.where(prow == 2 * pcol + g, 1.0, 0.0).astype(BF16), src[g]) for g in range(2))
        dst[...] = mix.astype(BF16)
    store_k = pltpu.make_async_copy(kout, kn_hbm, st_sem.at[0])
    store_v = pltpu.make_async_copy(vout, vn_hbm, st_sem.at[1])
    store_k.start()
    store_v.start()

    R = 3 * T
    coef = HD ** -0.5 * float(np.log2(np.e))
    q_tok = lax.rem(lax.broadcasted_iota(jnp.int32, (R, 1), 0), T)
    cl = lax.broadcasted_iota(jnp.int32, (R, HD), 1)
    lanes_kb = lax.broadcasted_iota(jnp.int32, (1, KB), 1)
    nb = KB // 128
    for g in range(2):
        q_g = qbuf[g]
        s_c = dot_t(q_g, kch[g])
        s_c = jnp.where(cl <= q_tok, s_c, -jnp.inf)

        def score(i, top):
            keys = kbuf[pl.ds(i * nb, nb), g * 128:(g + 1) * 128, :].reshape(KB, HD)
            s = dot_t(q_g, keys)
            off = lax.rem(lanes_kb + i * KB - start + 4 * window, window)
            off = jnp.where(start - window + off >= 0, off, -1)
            s = jnp.where(off > q_tok, s, -jnp.inf)
            sbuf[i] = s
            for j in range(nb):
                top = jnp.maximum(top, s[:, j * 128:(j + 1) * 128])
            return top

        top = lax.fori_loop(0, window // KB, score, s_c)
        top = jnp.max(top, axis=1, keepdims=True)
        e_c = jnp.exp2((s_c - top) * coef)

        def expo(i, mass):
            e = jnp.exp2((sbuf[i] - top) * coef)
            sbuf[i] = e
            for j in range(nb):
                mass = mass + e[:, j * 128:(j + 1) * 128]
            return mass

        mass = lax.fori_loop(0, window // KB, expo, e_c)
        scale = 1.0 / jnp.sum(mass, axis=1, keepdims=True)

        def weigh(i, acc):
            vals = vbuf[pl.ds(i * nb, nb), g * 128:(g + 1) * 128, :].reshape(KB, HD)
            return acc + dot((sbuf[i] * scale).astype(BF16), vals)

        acc = dot((e_c * scale).astype(BF16), vch[g])
        acc = lax.fori_loop(0, window // KB, weigh, acc)
        for j in range(3):
            head = 3 * g + j
            obuf[:, head * HD:(head + 1) * HD] = acc[j * T:(j + 1) * T].astype(BF16)

    loads[8].wait()
    mixed = obuf[...]
    sends = []
    for c in range(NCH):
        p = dot(mixed, wo[:, c * CW:(c + 1) * CW]).astype(BF16)
        part[c, 0] = p[:, :HW]
        part[c, 1] = p[:, HW:]
        cp = remote(part.at[c, 1 - core], rx1.at[c], s1.at[c], r1.at[c], partner)
        cp.start()
        sends.append(cp)
    hop2 = []
    for c in range(NCH):
        sends[c].wait_recv()
        cs[c] = (part[c, core].astype(F32) + rx1[c].astype(F32)).astype(BF16)
        cp = remote(cs.at[c], rx2.at[c], s2.at[c], r2.at[c], across)
        cp.start()
        hop2.append(cp)
    hop3 = []
    for c in range(NCH):
        hop2[c].wait_recv()
        cols = pl.ds(pl.multiple_of(c * CW + core * HW, 128), HW)
        total = cs[c].astype(F32) + rx2[c].astype(F32)
        hbuf[c, core] = (xall[:, cols].astype(F32) + total).astype(BF16)
        cp = remote(hbuf.at[c, core], hbuf.at[c, core], s3.at[c], r3.at[c], partner)
        cp.start()
        hop3.append(cp)
    sq = jnp.zeros((T, 1), F32)
    for c in range(NCH):
        hop3[c].wait_recv()
        for i in range(2):
            h32 = hbuf[c, i].astype(F32)
            sq = sq + jnp.sum(h32 * h32, axis=-1, keepdims=True)
    inv = lax.rsqrt(sq / D + NORM_EPS)
    for c in range(NCH):
        for i in range(2):
            lo = c * CW + i * HW
            nbuf[:, lo:lo + HW] = (hbuf[c, i].astype(F32) * inv * g2[:, lo:lo + HW].astype(F32)).astype(BF16)

    loads[9].wait()
    loads[10].wait()
    FB = 512
    F = wg.shape[1]

    def gate_up(j, carry):
        cols = pl.ds(pl.multiple_of(j * FB, FB), FB)
        m = nbuf[...]
        gate = dot(m, wg[:, cols])
        up = dot(m, wu[:, cols])
        ubuf[:, cols] = (gate * jax.nn.sigmoid(gate) * up).astype(BF16)
        return carry

    lax.fori_loop(0, F // FB, gate_up, 0)
    loads[11].wait()
    act = ubuf[...]
    hop4 = []
    for c in range(NCH):
        p = dot(act, wd[:, c * CW:(c + 1) * CW]).astype(BF16)
        for o in range(4):
            part2[c, o % 2, (o // 2) * tb:(o // 2 + 1) * tb] = p[o * tb:(o + 1) * tb]
        cp = remote(part2.at[c, 1 - core], rx4.at[c], s4.at[c], r4.at[c], partner)
        cp.start()
        hop4.append(cp)
    hop5 = []
    mine = rows_of(chip)
    theirs = rows_of(1 - chip)
    for c in range(NCH):
        hop4[c].wait_recv()
        cs2[c] = (part2[c, core, theirs].astype(F32) + rx4[c, theirs].astype(F32)).astype(BF16)
        cp = remote(cs2.at[c], rx5.at[c], s5.at[c], r5.at[c], across)
        cp.start()
        hop5.append(cp)
    outs = []
    for c in range(NCH):
        hop5[c].wait_recv()
        local = part2[c, core, mine].astype(F32) + rx4[c, mine].astype(F32) + rx5[c].astype(F32)
        for i in range(2):
            lo = c * CW + i * HW
            xout[:, lo:lo + HW] = (hbuf[c, i, rows_of(me)].astype(F32) + local[:, i * HW:(i + 1) * HW]).astype(BF16)
    store_x = pltpu.make_async_copy(xout, xo_hbm, st_sem.at[2])
    store_x.start()
    for cp in [to_partner, to_across, fwd] + sends + hop2 + hop3 + hop4 + hop5:
        cp.wait_send()
    store_k.wait()
    store_v.wait()
    store_x.wait()


def cache_kernel(start_ref, kc, vc, kch, vch, xin, kn, vn, xo, kbuf, vbuf, kcb, vcb, xb, in_sem, out_sem):
    nblk = kc.shape[0]
    per = kc.shape[1]
    rows = nblk * per
    small = [pltpu.make_async_copy(kch, kcb, in_sem.at[0, nblk]), pltpu.make_async_copy(vch, vcb, in_sem.at[1, nblk]),
             pltpu.make_async_copy(xin, xb, in_sem.at[2, nblk])]
    for cp in small:
        cp.start()
    reads = []
    for b in range(nblk):
        for i, (src, dst) in enumerate(((kc, kbuf), (vc, vbuf))):
            cp = pltpu.make_async_copy(src.at[b], dst.at[b], in_sem.at[i, b])
            cp.start()
            reads.append(cp)
    start = start_ref[0]
    for cp in small:
        cp.wait()
    xw = pltpu.make_async_copy(xb, xo, out_sem.at[2, 0])
    xw.start()
    first = lax.rem(2 * start, rows)
    writes = [xw]
    jrow = lax.broadcasted_iota(jnp.int32, (per, 128), 0)
    jcol = lax.broadcasted_iota(jnp.int32, (per, 128), 1)
    for b in range(nblk):
        for i in range(2):
            reads[2 * b + i].wait()
        lo = b * per
        ahead = lax.rem(lo - first + rows, rows)
        touched = (ahead < 128) | (ahead > rows - per)

        @pl.when(touched)
        def _():
            rel = lax.rem(jrow + lo - first + rows, rows)
            hot = jnp.where(rel == jcol, 1.0, 0.0).astype(BF16)
            inside = rel < 128
            kbuf[b] = jnp.where(inside, dot(hot, kcb[...]), kbuf[b].astype(F32)).astype(BF16)
            vbuf[b] = jnp.where(inside, dot(hot, vcb[...]), vbuf[b].astype(F32)).astype(BF16)

        for i, (src, dst) in enumerate(((kbuf, kn), (vbuf, vn))):
            cp = pltpu.make_async_copy(src.at[b], dst.at[b], out_sem.at[i, b])
            cp.start()
            writes.append(cp)
    for cp in writes:
        cp.wait()


def solution(mesh):
    row_spec = P('dp', 'tp', None)
    cache_spec = P('dp', None, 'tp', None)
    head_cols = P(None, 'tp', None)
    in_specs = (row_spec, P('dp'), cache_spec, cache_spec, P(), head_cols, head_cols, head_cols, P('tp', None, None), P(), P(None, 'tp'), P(None, 'tp'), P('tp', None))
    out_specs = (row_spec, cache_spec, cache_spec)

    def local_layer(x_in, start_pos, k_cache, v_cache, attn_gain, w_query, w_key, w_value, w_out, mlp_gain, w_gate, w_up, w_down):
        _, tb, D = x_in.shape
        T = 4 * tb
        window = k_cache.shape[1]
        F = w_gate.shape[1]
        CW = D // NCH
        HW = CW // 2
        qh = w_query.shape[1]
        invf = jnp.asarray(np.repeat(ROPE_BASE ** (-np.arange(0, HD, 2) / HD), 2).astype(np.float32)[None])
        blocks = window // 128
        kc = k_cache.reshape(blocks, 256, HD)
        vc = v_cache.reshape(blocks, 256, HD)
        wk = w_key.reshape(D // 128, 256, HD)
        wv = w_value.reshape(D // 128, 256, HD)
        any_spec = pl.BlockSpec(memory_space=pl.ANY)
        vmem = pltpu.VMEM
        dma = pltpu.SemaphoreType.DMA
        x_out, k_ch, v_ch = pl.pallas_call(
            layer_kernel,
            name='layer',
            out_shape=(jax.ShapeDtypeStruct((tb, D), BF16), jax.ShapeDtypeStruct((2 * T, HD), BF16), jax.ShapeDtypeStruct((2 * T, HD), BF16)),
            in_specs=[pl.BlockSpec(memory_space=pltpu.SMEM), pl.BlockSpec(memory_space=pltpu.VMEM)] + [any_spec] * 12,
            out_specs=(any_spec,) * 3,
            scratch_shapes=[
                vmem((T, D), BF16), vmem((T, D), BF16), vmem((1, D), BF16), vmem((1, D), BF16),
                vmem((blocks, 256, HD), BF16), vmem((blocks, 256, HD), BF16),
                vmem((qh, D, HD), BF16), vmem((D // 128, 256, HD), BF16), vmem((D // 128, 256, HD), BF16),
                vmem((qh * HD, D), BF16), vmem((D, F), BF16), vmem((D, F), BF16), vmem((F, D), BF16),
                vmem((window // KB, 3 * T, KB), F32), vmem((2, 3 * T, HD), BF16), vmem((2, 128, HD), BF16), vmem((2, 128, HD), BF16),
                vmem((T, qh * HD), BF16),
                vmem((NCH, 2, T, HW), BF16), vmem((NCH, T, HW), BF16), vmem((NCH, T, HW), BF16), vmem((NCH, T, HW), BF16),
                vmem((NCH, 2, T, HW), BF16), vmem((T, F), BF16),
                vmem((NCH, 2, 2 * tb, CW), BF16), vmem((NCH, 2 * tb, CW), BF16), vmem((NCH, tb, CW), BF16), vmem((NCH, tb, CW), BF16),
                vmem((tb, D), BF16), vmem((2 * T, HD), BF16), vmem((2 * T, HD), BF16),
                dma((12,)), dma((3,)), dma((3,)), dma((3,)),
            ] + [dma((NCH,))] * 10,
            compiler_params=pltpu.CompilerParams(collective_id=0, has_side_effects=True, vmem_limit_bytes=67043328),
        )(start_pos, invf, x_in.reshape(tb, D), attn_gain.reshape(1, D), mlp_gain.reshape(1, D), kc, vc, w_query.transpose(1, 0, 2), wk, wv,
          w_out.reshape(qh * HD, D), w_gate, w_up, w_down)
        nblk = 8
        per = 2 * window // nblk
        k_new, v_new, x_fin = pl.pallas_call(
            cache_kernel,
            name='cache',
            out_shape=(jax.ShapeDtypeStruct((nblk, per, HD), BF16),) * 2 + (jax.ShapeDtypeStruct((tb, D), BF16),),
            in_specs=[pl.BlockSpec(memory_space=pltpu.SMEM)] + [any_spec] * 5,
            out_specs=(any_spec,) * 3,
            scratch_shapes=[vmem((nblk, per, HD), BF16)] * 2 + [vmem((2 * T, HD), BF16)] * 2 + [vmem((tb, D), BF16), dma((3, nblk + 1)), dma((3, nblk))],
        )(start_pos, k_cache.reshape(nblk, per, HD), v_cache.reshape(nblk, per, HD), k_ch, v_ch, x_out)
        return x_fin.reshape(x_in.shape), k_new.reshape(k_cache.shape), v_new.reshape(v_cache.shape)

    return jax.shard_map(local_layer, mesh=mesh, in_specs=in_specs, out_specs=out_specs, check_vma=False)
```

time: 163 us -> 50.4 us (0.31)
  other arithmetic: 57.7 us -> 0 us
  Pallas kernels: 0 us -> 46.4 us
  matrix products: 35.9 us -> 0 us
  blocking collectives: 19.9 us -> 0 us
  local copies, waits for them, and re-layouts: 18.1 us -> 2.6 us
  waiting for transfers between devices: 15.2 us -> 0 us
  between operations: 15.2 us -> 1.29 us
    select_n x2 -> x0, other arithmetic: 49.8 us -> none  [the longest x1 49.8 us: one_row(): return jnp.where((offsets < chunk_len)[:, None, None], placed, old_rows)]
    pallas_call x0 -> x2, Pallas kernels: none -> 46.4 us  [the longest x1 42.3 us: local_layer(): pl.pallas_call(layer_kernel, name='layer', out_shape=(jax.ShapeDtypeStruc...]
    dot_general x10 -> x0, matrix products: 35.9 us -> none  [the longest x1 13.4 us: local_layer(): jnp.einsum('btf,fd->btd', activated, w_down, preferred_element_type=jnp.f...]
    all_gather x2 -> x0, blocking collectives: 19.9 us -> none  [the longest x1 11.3 us: local_layer(): lax.all_gather(rms_norm(x_in, attn_gain), 'tp', axis=1, tiled=True)]
    reduce_scatter x2 -> x0, waiting for transfers between devices: 15.2 us -> none  [the longest x1 15.2 us: local_layer(): lax.psum_scatter(attn_part, 'tp', scatter_dimension=1, tiled=True)]
    reshape x1 -> x2, local copies, waits for them, and re-layouts: 12.6 us -> 2.6 us  [the longest x1 1.3 us: local_layer(): attn_gain.reshape(1, D)]
    convert_element_type x7 -> x0, other arithmetic: 4.27 us -> none  [the longest x4 2.68 us: rms_norm(): return (rows32 * inv_rms * gain.astype(jnp.float32)).astype(jnp.bfloat16)]
    dot_general x1 -> x0, local copies, waits for them, and re-layouts: 3.69 us -> none  [project_qkv(): jnp.einsum('btd,dke->btke', normed, w_key, preferred_element_type=jnp.flo...]
  transfers between devices with their start and end apart: 2 -> 0, of which waited for: 1 -> 0; matrix products, arithmetic and copies ran while one was open for 31% -> 0% of each run, Pallas kernels for 0% -> 0%
where the time goes in v1:
time: 50.4 us; the launch traced here: 50.3 us
  Pallas kernels  46.4 us (92%)
  local copies, waits for them, and re-layouts  2.6 us (5%)
  between operations  1.29 us (3%)
    pallas_call x1, Pallas kernels, local_layer(): pl.pallas_call(layer_kernel, name='layer', out_shape=(jax.ShapeDtypeStruc...  42.3 us
    pallas_call x1, Pallas kernels, local_layer(): pl.pallas_call(cache_kernel, name='cache', out_shape=(jax.ShapeDtypeStruc...  4.06 us
    reshape x1, local copies, waits for them, and re-layouts, local_layer(): attn_gain.reshape(1, D)  1.3 us
    reshape x1, local copies, waits for them, and re-layouts, local_layer(): mlp_gain.reshape(1, D)  1.3 us

profile of v1, /device:TPU:0, one launch (start us, length us, event | category | flops | bytes accessed | tf_op | source)
XLA Modules:
  0.0 50.3 jit_solution(1570006928103328960)
XLA Ops:
  1.3 1.3 %reshape.48.g1_hbm = bf16[1,3072]{1,0:T(2,128)(2,1)} reshape(bf16[3072]{0:T(1024)(128)(2,1)} %param.18) | data formatting | bytes 12288 | tf_op jit(solution)/shard_map/reshape | solution.py:370
  2.6 1.3 %reshape.49.g2_hbm = bf16[1,3072]{1,0:T(2,128)(2,1)} reshape(bf16[3072]{0:T(1024)(128)(2,1)} %param.23) | data formatting | bytes 12288 | tf_op jit(solution)/shard_map/reshape | solution.py:370
  3.9 42.3 %layer.1 = (bf16[16,3072]{1,0:T(8,128)(2,1)}, bf16[128,128]{1,0:T(8,128)(2,1)}, bf16[128,128]{1,0:T(8,128)(2,1)}) custom-call(s32[1]{0:T(128)S(6)} %copy.17.start_ref, f32[1,128]{1,0:T(1,128)} %constant.2.clone.invf_ref, bf16[16,3072]{1,0:T(8,128)(2,1)} %bitcast.20, bf16[1,3072]{1,0:T(2,128)(2,1)} %reshape.48.g1_hbm, bf16[1,3072]{1,0:T(2,128)(2,1)} %reshape.49.g2_hbm, ...), custom_call_target="tpu_custom_call" | custom-call | tf_op jit(solution)/shard_map/layer/pallas_call | solution.py:350
  46.2 4.1 %cache.1 = (bf16[8,1024,128]{2,1,0:T(8,128)(2,1)}, bf16[8,1024,128]{2,1,0:T(8,128)(2,1)}, bf16[16,3072]{1,0:T(8,128)(2,1)}) custom-call(s32[1]{0:T(128)S(6)} %copy.17.start_ref, bf16[8,1024,128]{2,1,0:T(8,128)(2,1)} %bitcast.13, bf16[8,1024,128]{2,1,0:T(8,128)(2,1)} %bitcast.15, bf16[128,128]{1,0:T(8,128)(2,1)} %get-tuple-element.9.kch, ...), custom_call_target="tpu_custom_call" | custom-call | tf_op jit(solution)/shard_map/cache/pallas_call | solution.py:374

commit v2 on v1

v2 whole, which is shorter than its diff:
```python
import functools

import jax
import jax.numpy as jnp
import numpy as np
from jax import lax
from jax.experimental import pallas as pl
from jax.experimental.pallas import tpu as pltpu
from jax.sharding import PartitionSpec as P

ROPE_BASE = 10000.0
NORM_EPS = 1e-5
MESH = pl.DeviceIdType.MESH
BF16 = jnp.bfloat16
F32 = jnp.float32
HD = 128
NCH = 6
NCH2 = 6
NAG = 4
LAG = 4
KB = 512


def dot(a, b):
    return jnp.dot(a, b, preferred_element_type=F32)


def dot_t(a, b):
    return lax.dot_general(a, b, (((1,), (1,)), ((), ())), preferred_element_type=F32)


class Phases:
    def __init__(self):
        self.scope = None

    def __call__(self, name):
        self.close()
        self.scope = jax.named_scope(name)
        self.scope.__enter__()

    def close(self):
        if self.scope is not None:
            self.scope.__exit__(None, None, None)
        self.scope = None


def layer_kernel(start_hbm, invf_hbm, x_hbm, g1_hbm, g2_hbm, kc_hbm, vc_hbm, wq_hbm, wk_hbm, wv_hbm, wo_hbm, wg_hbm, wu_hbm, wd_hbm,
                 xo_hbm, kn_hbm, vn_hbm,
                 start_s, invf, xown, xh, nbuf, g1, g2, kbuf, vbuf, wq, wk, wv, wo, wg, wu, wd,
                 qacc, offb, sbuf, qbuf, kch, vch, obuf, part, rx1, cs, rx2, hbuf, gacc, ubuf, part2, rx4, cs2, rx5, xout, kout, vout,
                 ld_sem, st_sem, agp_s, agp_r, aga_s, aga_r, agf_s, agf_r, xs_s, xs_r, s1, r1, s2, r2, s3, r3, s4, r4, s5, r5):
    phase = Phases()
    phase('entry')
    T, D = nbuf.shape
    half = D // 2
    HW = half // NCH
    CW = D // NCH2
    AW = D // NAG
    tb = T // 4
    window = kbuf.shape[0] * 128
    F = wg.shape[1]
    me = lax.axis_index('tp')
    core = lax.rem(me, 2)
    chip = lax.div(me, 2)
    partner = chip * 2 + (1 - core)
    across = (1 - chip) * 2 + core
    diag = (1 - chip) * 2 + (1 - core)

    def load(i, src, dst):
        return pltpu.make_async_copy(src, dst, ld_sem.at[i])

    def rows_of(owner):
        return pl.ds(pl.multiple_of(owner * tb, tb), tb)

    def half_of(which):
        return pl.ds(pl.multiple_of(which * half, 128), half)

    def remote(src, dst, send, recv, dev):
        return pltpu.make_async_remote_copy(src_ref=src, dst_ref=dst, send_sem=send, recv_sem=recv, device_id={'tp': dev}, device_id_type=MESH)

    def wide(gain, lo, n):
        return jnp.concatenate([gain[i:i + 1] for i in range(lo // HD, (lo + n) // HD)], axis=1)

    barrier = pltpu.get_barrier_semaphore()
    for other in (across, diag, partner):
        pl.semaphore_signal(barrier, inc=1, device_id={'tp': other}, device_id_type=MESH)

    own = rows_of(me)
    loads = [load(0, x_hbm, xown), load(1, g1_hbm, g1), load(2, g2_hbm, g2), load(12, start_hbm, start_s), load(13, invf_hbm, invf),
             load(14, x_hbm.at[:, half_of(core)], xh.at[own]),
             load(3, kc_hbm, kbuf), load(4, vc_hbm, vbuf),
             load(5, wk_hbm, wk), load(6, wv_hbm, wv), load(7, wq_hbm, wq), load(8, wo_hbm, wo), load(9, wg_hbm, wg),
             load(10, wu_hbm, wu), load(11, wd_hbm, wd)]
    (ld_x, ld_g1, ld_g2, ld_start, ld_invf, ld_xh, ld_kc, ld_vc, ld_wk, ld_wv, ld_wq, ld_wo, ld_wg, ld_wu, ld_wd) = loads
    for item in loads:
        item.start()

    ld_x.wait()
    ld_g1.wait()
    x32 = xown[...].astype(F32)
    inv = lax.rsqrt(jnp.mean(x32 * x32, axis=-1, keepdims=True) + NORM_EPS)
    nbuf[own] = (x32 * inv * wide(g1[...].astype(F32), 0, D)).astype(BF16)
    pl.semaphore_wait(barrier, 3)
    ag_a = []
    for c in range(NAG):
        piece = nbuf.at[own, pl.ds(c * AW, AW)]
        ag_a.append(remote(piece, piece, aga_s.at[c], aga_r.at[c], across))
        ag_a[c].start()
    ag_p = remote(nbuf.at[own], nbuf.at[own], agp_s.at[0], agp_r.at[0], partner)
    ag_p.start()

    row = lax.broadcasted_iota(jnp.int32, (256, 256), 0)
    col = lax.broadcasted_iota(jnp.int32, (256, 256), 1)
    pick = jnp.where(col == 2 * lax.rem(row, 128) + lax.div(row, 128), 1.0, 0.0).astype(BF16)

    def split(a_ref, b_ref, lo, hi):
        def body(b, carry):
            both = jnp.concatenate([a_ref[b], b_ref[b]], axis=1)
            sep = dot(pick, both).astype(BF16)
            a_ref[b] = sep[:, :128]
            b_ref[b] = sep[:, 128:]
            return carry
        lax.fori_loop(lo, hi, body, 0, unroll=min(8, hi - lo))

    phase('wait_cache')
    ld_kc.wait()
    ld_vc.wait()
    phase('split_cache')
    split(kbuf, vbuf, 0, kbuf.shape[0])
    phase('wait_wkv')
    ld_wk.wait()
    ld_wv.wait()
    ag_f = []
    per_ag = wk.shape[0] // NAG
    for c in range(NAG):
        phase(f'wait_across{c}')
        ag_a[c].wait_recv()
        piece = nbuf.at[rows_of(across), pl.ds(c * AW, AW)]
        ag_f.append(remote(piece, piece, agf_s.at[c], agf_r.at[c], partner))
        ag_f[c].start()
        phase(f'split_wkv{c}')
        split(wk, wv, c * per_ag, (c + 1) * per_ag)

    x_sends = [remote(xown.at[:, half_of(core)], xh.at[own], xs_s.at[0], xs_r.at[0], across),
               remote(xown.at[:, half_of(1 - core)], xh.at[own], xs_s.at[1], xs_r.at[1], diag),
               remote(xown.at[:, half_of(1 - core)], xh.at[own], xs_s.at[2], xs_r.at[2], partner)]
    for cp in x_sends:
        cp.start()

    phase('trig')
    ld_start.wait()
    ld_invf.wait()
    start = start_s[0]
    lane = lax.broadcasted_iota(jnp.int32, (T, HD), 1)
    tok = lax.broadcasted_iota(jnp.int32, (T, HD), 0)
    angles = (start + tok).astype(F32) * invf[...]
    cos_t = jnp.cos(angles)
    even = lax.rem(lane, 2) == 0
    sin_t = jnp.sin(angles)
    sin_t = jnp.where(even, -sin_t, sin_t)
    slot = lax.broadcasted_iota(jnp.int32, (8, window), 1)
    off = lax.rem(slot - start + 4 * window, window)
    offb[...] = jnp.where(start - window + off >= 0, off, -1)

    def rope(h):
        swapped = jnp.where(even, pltpu.roll(h, HD - 1, 1), pltpu.roll(h, 1, 1))
        return h * cos_t + swapped * sin_t

    def split_rows(ref, g, c):
        return ref[c * per_ag:(c + 1) * per_ag, g * 128:(g + 1) * 128, :].reshape(AW, HD)

    ag_p.wait_recv()
    ld_wq.wait()
    kch[...] = jnp.zeros_like(kch)
    vch[...] = jnp.zeros_like(vch)
    for c in range(NAG):
        phase(f'wait_fwd{c}')
        ag_f[c].wait_recv()
        phase(f'qkv{c}')
        rows = nbuf[:, c * AW:(c + 1) * AW]
        for o in range(5):
            if o < 3:
                w = jnp.concatenate([wq[2 * o, c * AW:(c + 1) * AW], wq[2 * o + 1, c * AW:(c + 1) * AW]], axis=1)
            else:
                ref = wk if o == 3 else wv
                w = jnp.concatenate([split_rows(ref, 0, c), split_rows(ref, 1, c)], axis=1)
            p = dot(rows, w)
            qacc[o] = p if c == 0 else qacc[o] + p
    phase('rope')
    for g in range(2):
        kch[g, :T] = rope(qacc[3, :, g * HD:(g + 1) * HD]).astype(BF16)
        vch[g, :T] = qacc[4, :, g * HD:(g + 1) * HD].astype(BF16)
    for head in range(6):
        qbuf[head // 3, (head % 3) * T:(head % 3 + 1) * T] = rope(qacc[head // 2, :, (head % 2) * HD:(head % 2 + 1) * HD]).astype(BF16)

    phase('kvout')
    prow = lax.broadcasted_iota(jnp.int32, (2 * T, HD), 0)
    pcol = lax.broadcasted_iota(jnp.int32, (2 * T, HD), 1)
    for src, dst in ((kch, kout), (vch, vout)):
        mix = sum(dot(jnp.where(prow == 2 * pcol + g, 1.0, 0.0).astype(BF16), src[g]) for g in range(2))
        dst[...] = mix.astype(BF16)
    store_k = pltpu.make_async_copy(kout, kn_hbm, st_sem.at[0])
    store_v = pltpu.make_async_copy(vout, vn_hbm, st_sem.at[1])
    store_k.start()
    store_v.start()

    phase('attn')
    coef = HD ** -0.5 * float(np.log2(np.e))
    nblk = window // KB
    nb = KB // 128
    q_tok = lax.broadcasted_iota(jnp.int32, (T, HD), 0)
    q_tok3 = q_tok.reshape(T // 8, 8, HD)
    k_idx = lax.broadcasted_iota(jnp.int32, (T, HD), 1)

    def blocks(ref, g, i):
        return ref[i * nb:(i + 1) * nb, g * 128:(g + 1) * 128, :].reshape(KB, HD)

    top, mass, s_c = [[None] * 3, [None] * 3], [[None] * 3, [None] * 3], [[None] * 3, [None] * 3]
    peak, e_c, scale, acc = [[None] * 3, [None] * 3], [[None] * 3, [None] * 3], [[None] * 3, [None] * 3], [None, None]

    def score_chunk(g):
        s = dot_t(qbuf[g], kch[g])
        for h in range(3):
            s_c[g][h] = jnp.where(k_idx <= q_tok, s[h * T:(h + 1) * T], -jnp.inf)
            top[g][h] = s_c[g][h]

    def score(g, i):
        s = dot_t(qbuf[g], blocks(kbuf, g, i))
        for j in range(nb):
            o = offb[:, i * KB + j * 128:i * KB + (j + 1) * 128][None]
            keep = o > q_tok3
            for h in range(3):
                piece = s[h * T:(h + 1) * T, j * 128:(j + 1) * 128].reshape(T // 8, 8, HD)
                piece = jnp.where(keep, piece, -jnp.inf).reshape(T, HD)
                sbuf[g, i, h * T:(h + 1) * T, j * 128:(j + 1) * 128] = piece
                top[g][h] = jnp.maximum(top[g][h], piece)

    def expo_chunk(g):
        for h in range(3):
            peak[g][h] = jnp.max(top[g][h], axis=1, keepdims=True)
            e_c[g][h] = jnp.exp2((s_c[g][h] - peak[g][h]) * coef)
            mass[g][h] = e_c[g][h]

    def expo(g, h, i):
        e = jnp.exp2((sbuf[g, i, h * T:(h + 1) * T] - peak[g][h]) * coef)
        sbuf[g, i, h * T:(h + 1) * T] = e
        for j in range(nb):
            mass[g][h] = mass[g][h] + e[:, j * 128:(j + 1) * 128]

    def weigh_chunk(g):
        for h in range(3):
            scale[g][h] = 1.0 / jnp.sum(mass[g][h], axis=1, keepdims=True)
        p = jnp.concatenate([(e_c[g][h] * scale[g][h]).astype(BF16) for h in range(3)], axis=0)
        acc[g] = dot(p, vch[g])

    def weigh(g, i):
        p = jnp.concatenate([(sbuf[g, i, h * T:(h + 1) * T] * scale[g][h]).astype(BF16) for h in range(3)], axis=0)
        acc[g] = acc[g] + dot(p, blocks(vbuf, g, i))

    order = [(h, i) for h in range(3) for i in range(nblk)]
    score_chunk(0)
    for i in range(nblk):
        score(0, i)
    score_chunk(1)
    expo_chunk(0)
    for i in range(nblk):
        score(1, i)
        for h, k in order[3 * i:3 * i + 3]:
            expo(0, h, k)
    expo_chunk(1)
    weigh_chunk(0)
    for i in range(nblk):
        weigh(0, i)
        for h, k in order[3 * i:3 * i + 3]:
            expo(1, h, k)
    weigh_chunk(1)
    for i in range(nblk):
        weigh(1, i)
    for g in range(2):
        for h in range(3):
            head = 3 * g + h
            obuf[:, head * HD:(head + 1) * HD] = acc[g][h * T:(h + 1) * T].astype(BF16)

    phase('oproj')
    ld_wo.wait()
    hop1, hop2, hop3, hop4, hop5 = [], [], [], [], []
    for c in range(NCH):
        for i in range(2):
            lo = i * half + c * HW
            part[c, i] = dot(obuf[...], wo[:, lo:lo + HW]).astype(BF16)
        hop1.append(remote(part.at[c, 1 - core], rx1.at[c], s1.at[c], r1.at[c], partner))
        hop1[c].start()
    phase('hop1')
    for c in range(NCH):
        hop1[c].wait_recv()
        cs[c] = (part[c, core].astype(F32) + rx1[c].astype(F32)).astype(BF16)
        hop2.append(remote(cs.at[c], rx2.at[c], s2.at[c], r2.at[c], across))
        hop2[c].start()

    phase('hop2')
    for cp in x_sends:
        cp.wait_recv()
    ld_xh.wait()
    ld_g2.wait()
    gain2 = g2[...].astype(F32)
    g_top = jnp.maximum(jnp.max(jnp.max(jnp.abs(gain2), axis=1, keepdims=True), axis=0, keepdims=True), 1e-30)
    gain2 = gain2 / g_top
    ld_wg.wait()
    ld_wu.wait()
    squares = []

    def gate_up(c):
        hop3[c].wait_recv()
        phase(f'gateup{c}')
        lhs = []
        for i in range(2):
            h32 = hbuf[c, i].astype(F32)
            lhs.append((h32 * wide(gain2, i * half + c * HW, HW)).astype(BF16))
            for j in range(HW // 128):
                piece = h32[:, j * 128:(j + 1) * 128]
                squares.append(piece * piece if not squares else squares.pop() + piece * piece)
        for k, w in enumerate((wg, wu)):
            for lo in range(0, F, 512):
                p = sum(dot(lhs[i], w[i * half + c * HW:i * half + (c + 1) * HW, lo:lo + 512]) for i in range(2))
                gacc[k, :, lo:lo + 512] = p if c == 0 else gacc[k, :, lo:lo + 512] + p

    for c in range(NCH):
        phase(f'hop2_{c}')
        hop2[c].wait_recv()
        total = cs[c].astype(F32) + rx2[c].astype(F32)
        hbuf[c, core] = (xh[:, c * HW:(c + 1) * HW].astype(F32) + total).astype(BF16)
        hop3.append(remote(hbuf.at[c, core], hbuf.at[c, core], s3.at[c], r3.at[c], partner))
        hop3[c].start()
        if c >= 2:
            gate_up(c - 2)
    for c in range(NCH - 2, NCH):
        phase(f'hop3_{c}')
        gate_up(c)
    phase('act')
    inv2 = lax.rsqrt(jnp.sum(squares[0], axis=-1, keepdims=True) / D + NORM_EPS)
    inv2 = inv2 * g_top
    gate = jnp.where(inv2 > 0, gacc[0] * inv2, 0.0)
    up = jnp.where(inv2 > 0, gacc[1] * inv2, 0.0)
    ubuf[...] = (gate * jax.nn.sigmoid(gate) * up).astype(BF16)

    phase('down')
    ld_wd.wait()
    mine = rows_of(chip)
    theirs = rows_of(1 - chip)

    def chip_sum(c):
        hop4[c].wait_recv()
        cs2[c] = (part2[c, core, theirs].astype(F32) + rx4[c, theirs].astype(F32)).astype(BF16)
        hop5.append(remote(cs2.at[c], rx5.at[c], s5.at[c], r5.at[c], across))
        hop5[c].start()

    for c in range(NCH2):
        p = dot(ubuf[...], wd[:, c * CW:(c + 1) * CW]).astype(BF16)
        for o in range(4):
            part2[c, o % 2, (o // 2) * tb:(o // 2 + 1) * tb] = p[o * tb:(o + 1) * tb]
        hop4.append(remote(part2.at[c, 1 - core], rx4.at[c], s4.at[c], r4.at[c], partner))
        hop4[c].start()
        if c >= LAG:
            chip_sum(c - LAG)
    phase('hop4')
    for c in range(NCH2 - LAG, NCH2):
        chip_sum(c)
    phase('hop5')
    for c in range(NCH2):
        hop5[c].wait_recv()
        local = part2[c, core, mine].astype(F32) + rx4[c, mine].astype(F32) + rx5[c].astype(F32)
        for j in range(CW // HW):
            lo = c * CW + j * HW
            h_own = hbuf[(lo % half) // HW, lo // half, own].astype(F32)
            xout[:, lo:lo + HW] = (h_own + local[:, j * HW:(j + 1) * HW]).astype(BF16)
    store_x = pltpu.make_async_copy(xout, xo_hbm, st_sem.at[2])
    phase('fin')
    store_x.start()
    for cp in ag_a + [ag_p] + ag_f + x_sends + hop1 + hop2 + hop3 + hop4 + hop5:
        cp.wait_send()
    store_k.wait()
    store_v.wait()
    store_x.wait()
    phase.close()


def cache_kernel(start_ref, kc, vc, kch, vch, xin, kn, vn, xo, kbuf, vbuf, kcb, vcb, xb, in_sem, out_sem):
    nblk = kc.shape[0]
    per = kc.shape[1]
    rows = nblk * per
    small = [pltpu.make_async_copy(kch, kcb, in_sem.at[0, nblk]), pltpu.make_async_copy(vch, vcb, in_sem.at[1, nblk]),
             pltpu.make_async_copy(xin, xb, in_sem.at[2, nblk])]
    for cp in small:
        cp.start()
    reads = []
    for b in range(nblk):
        for i, (src, dst) in enumerate(((kc, kbuf), (vc, vbuf))):
            cp = pltpu.make_async_copy(src.at[b], dst.at[b], in_sem.at[i, b])
            cp.start()
            reads.append(cp)
    start = start_ref[0]
    for cp in small:
        cp.wait()
    xw = pltpu.make_async_copy(xb, xo, out_sem.at[2, 0])
    xw.start()
    first = lax.rem(2 * start, rows)
    writes = [xw]
    jrow = lax.broadcasted_iota(jnp.int32, (per, 128), 0)
    jcol = lax.broadcasted_iota(jnp.int32, (per, 128), 1)
    for b in range(nblk):
        for i in range(2):
            reads[2 * b + i].wait()
        lo = b * per
        ahead = lax.rem(lo - first + rows, rows)
        touched = (ahead < 128) | (ahead > rows - per)

        @pl.when(touched)
        def _():
            rel = lax.rem(jrow + lo - first + rows, rows)
            hot = jnp.where(rel == jcol, 1.0, 0.0).astype(BF16)
            inside = rel < 128
            kbuf[b] = jnp.where(inside, dot(hot, kcb[...]), kbuf[b].astype(F32)).astype(BF16)
            vbuf[b] = jnp.where(inside, dot(hot, vcb[...]), vbuf[b].astype(F32)).astype(BF16)

        for i, (src, dst) in enumerate(((kbuf, kn), (vbuf, vn))):
            cp = pltpu.make_async_copy(src.at[b], dst.at[b], out_sem.at[i, b])
            cp.start()
            writes.append(cp)
    for cp in writes:
        cp.wait()


def solution(mesh):
    row_spec = P('dp', 'tp', None)
    cache_spec = P('dp', None, 'tp', None)
    head_cols = P(None, 'tp', None)
    in_specs = (row_spec, P('dp'), cache_spec, cache_spec, P(), head_cols, head_cols, head_cols, P('tp', None, None), P(), P(None, 'tp'), P(None, 'tp'), P('tp', None))
    out_specs = (row_spec, cache_spec, cache_spec)

    def local_layer(x_in, start_pos, k_cache, v_cache, attn_gain, w_query, w_key, w_value, w_out, mlp_gain, w_gate, w_up, w_down):
        _, tb, D = x_in.shape
        T = 4 * tb
        window = k_cache.shape[1]
        F = w_gate.shape[1]
        HW = D // 2 // NCH
        CW = D // NCH2
        qh = w_query.shape[1]
        invf = jnp.asarray(np.repeat(ROPE_BASE ** (-np.arange(0, HD, 2) / HD), 2).astype(np.float32)[None])
        blocks = window // 128
        kc = k_cache.reshape(blocks, 256, HD)
        vc = v_cache.reshape(blocks, 256, HD)
        wk = w_key.reshape(D // 128, 256, HD)
        wv = w_value.reshape(D // 128, 256, HD)
        any_spec = pl.BlockSpec(memory_space=pl.ANY)
        vmem = pltpu.VMEM
        dma = pltpu.SemaphoreType.DMA
        x_out, k_ch, v_ch = pl.pallas_call(
            layer_kernel,
            name='layer',
            out_shape=(jax.ShapeDtypeStruct((tb, D), BF16), jax.ShapeDtypeStruct((2 * T, HD), BF16), jax.ShapeDtypeStruct((2 * T, HD), BF16)),
            in_specs=[any_spec] * 14,
            out_specs=(any_spec,) * 3,
            scratch_shapes=[
                pltpu.SMEM((1,), jnp.int32), vmem((1, HD), F32),
                vmem((tb, D), BF16), vmem((T, D // 2), BF16), vmem((T, D), BF16), vmem((D // HD, HD), BF16), vmem((D // HD, HD), BF16),
                vmem((blocks, 256, HD), BF16), vmem((blocks, 256, HD), BF16),
                vmem((qh, D, HD), BF16), vmem((D // 128, 256, HD), BF16), vmem((D // 128, 256, HD), BF16),
                vmem((qh * HD, D), BF16), vmem((D, F), BF16), vmem((D, F), BF16), vmem((F, D), BF16),
                vmem((5, T, 256), F32), vmem((8, window), jnp.int32),
                vmem((2, window // KB, 3 * T, KB), F32), vmem((2, 3 * T, HD), BF16), vmem((2, 128, HD), BF16), vmem((2, 128, HD), BF16),
                vmem((T, qh * HD), BF16),
                vmem((NCH, 2, T, HW), BF16), vmem((NCH, T, HW), BF16), vmem((NCH, T, HW), BF16), vmem((NCH, T, HW), BF16),
                vmem((NCH, 2, T, HW), BF16), vmem((2, T, F), F32), vmem((T, F), BF16),
                vmem((NCH2, 2, 2 * tb, CW), BF16), vmem((NCH2, 2 * tb, CW), BF16), vmem((NCH2, tb, CW), BF16), vmem((NCH2, tb, CW), BF16),
                vmem((tb, D), BF16), vmem((2 * T, HD), BF16), vmem((2 * T, HD), BF16),
                dma((15,)), dma((3,)), dma((1,)), dma((1,))] + [dma((NAG,))] * 4 + [dma((3,))] * 2 + [dma((NCH,))] * 6 + [dma((NCH2,))] * 4,
            compiler_params=pltpu.CompilerParams(collective_id=0, has_side_effects=True, vmem_limit_bytes=67043328),
        )(start_pos, invf, x_in.reshape(tb, D), attn_gain.reshape(D // HD, HD), mlp_gain.reshape(D // HD, HD), kc, vc, w_query.transpose(1, 0, 2), wk, wv,
          w_out.reshape(qh * HD, D), w_gate, w_up, w_down)
        nblk = 8
        per = 2 * window // nblk
        k_new, v_new, x_fin = pl.pallas_call(
            cache_kernel,
            name='cache',
            out_shape=(jax.ShapeDtypeStruct((nblk, per, HD), BF16),) * 2 + (jax.ShapeDtypeStruct((tb, D), BF16),),
            in_specs=[pl.BlockSpec(memory_space=pltpu.SMEM)] + [any_spec] * 5,
            out_specs=(any_spec,) * 3,
            scratch_shapes=[vmem((nblk, per, HD), BF16)] * 2 + [vmem((2 * T, HD), BF16)] * 2 + [vmem((tb, D), BF16), dma((3, nblk + 1)), dma((3, nblk))],
        )(start_pos, k_cache.reshape(nblk, per, HD), v_cache.reshape(nblk, per, HD), k_ch, v_ch, x_out)
        return x_fin.reshape(x_in.shape), k_new.reshape(k_cache.shape), v_new.reshape(v_cache.shape)

    return jax.shard_map(local_layer, mesh=mesh, in_specs=in_specs, out_specs=out_specs, check_vma=False)
```

time: 50.4 us -> 37.3 us (0.74)
  Pallas kernels: 46.4 us -> 36 us
  local copies, waits for them, and re-layouts: 2.6 us -> 0 us
    pallas_call x1, Pallas kernels: 42.3 us -> 31.9 us  [local_layer(): pl.pallas_call(layer_kernel, name='layer', out_shape=(jax.ShapeDtypeStruc...]
    reshape x2 -> x0, local copies, waits for them, and re-layouts: 2.6 us -> none  [the longest x1 1.3 us: local_layer(): attn_gain.reshape(1, D)]
where the time goes in v2:
time: 37.3 us
  Pallas kernels  36 us (97%)
  between operations  1.29 us (3%)
    pallas_call x1, Pallas kernels, local_layer(): pl.pallas_call(layer_kernel, name='layer', out_shape=(jax.ShapeDtypeStruc...  31.9 us
    pallas_call x1, Pallas kernels, local_layer(): pl.pallas_call(cache_kernel, name='cache', out_shape=(jax.ShapeDtypeStruc...  4.06 us

profile of v2, /device:TPU:0, one launch (start us, length us, event | category | flops | bytes accessed | tf_op | source)
XLA Modules:
  0.0 37.3 jit_solution(18228656233634069798)
XLA Ops:
  1.3 31.9 %layer.1 = (bf16[16,3072]{1,0:T(8,128)(2,1)}, bf16[128,128]{1,0:T(8,128)(2,1)}, bf16[128,128]{1,0:T(8,128)(2,1)}) custom-call(s32[1]{0:T(128)S(6)} %copy.17.start_hbm.start_ref, f32[1,128]{1,0:T(1,128)} %constant.2.clone.invf_hbm, bf16[16,3072]{1,0:T(8,128)(2,1)} %bitcast.22, bf16[24,128]{1,0:T(8,128)(2,1)} %bitcast.23, bf16[24,128]{1,0:T(8,128)(2,1)} %bitcast.24, ...), custom_call_target="tpu_custom_call" | custom-call | tf_op jit(solution)/shard_map/layer/pallas_call | solution.py:457
  33.2 4.1 %cache.1 = (bf16[8,1024,128]{2,1,0:T(8,128)(2,1)}, bf16[8,1024,128]{2,1,0:T(8,128)(2,1)}, bf16[16,3072]{1,0:T(8,128)(2,1)}) custom-call(s32[1]{0:T(128)S(6)} %copy.17.start_hbm.start_ref, bf16[8,1024,128]{2,1,0:T(8,128)(2,1)} %bitcast.15, bf16[8,1024,128]{2,1,0:T(8,128)(2,1)} %bitcast.17, bf16[128,128]{1,0:T(8,128)(2,1)} %get-tuple-element.9.kch, ...), custom_call_target="tpu_custom_call" | custom-call | tf_op jit(solution)/shard_map/cache/pallas_call | solution.py:482

commit v3 on v2

--- a/solution.py
+++ b/solution.py
@@ -17,12 +17,22 @@
 NCH = 6
 NCH2 = 6
 NAG = 4
-LAG = 4
+LAG = 2
 KB = 512
+SLAB = 256
+LAYER_VMEM = 62 * 10**6
+CACHE_VMEM = 24 * 10**6
+SPARE = 3 * 2**23
 
 
 def dot(a, b):
     return jnp.dot(a, b, preferred_element_type=F32)
+
+
+def dot_padded(a, b):
+    p = dot(a, b)
+    m = a.shape[0] // 2
+    return p[:m] + p[m:]
 
 
 def dot_t(a, b):
@@ -48,7 +58,7 @@
                  xo_hbm, kn_hbm, vn_hbm,
                  start_s, invf, xown, xh, nbuf, g1, g2, kbuf, vbuf, wq, wk, wv, wo, wg, wu, wd,
                  qacc, offb, sbuf, qbuf, kch, vch, obuf, part, rx1, cs, rx2, hbuf, gacc, ubuf, part2, rx4, cs2, rx5, xout, kout, vout,
-                 ld_sem, st_sem, agp_s, agp_r, aga_s, aga_r, agf_s, agf_r, xs_s, xs_r, s1, r1, s2, r2, s3, r3, s4, r4, s5, r5):
+                 ld_sem, st_sem, out_sem, agp_r, aga_r, agf_r, xs_r, r1, r2, r3, r4, r5):
     phase = Phases()
     phase('entry')
     T, D = nbuf.shape
@@ -58,7 +68,7 @@
     AW = D // NAG
     tb = T // 4
     window = kbuf.shape[0] * 128
-    F = wg.shape[1]
+    F = wg.shape[0] * SLAB
     me = lax.axis_index('tp')
     core = lax.rem(me, 2)
     chip = lax.div(me, 2)
@@ -69,14 +79,21 @@
     def load(i, src, dst):
         return pltpu.make_async_copy(src, dst, ld_sem.at[i])
 
+    def slabs(i, src, dst):
+        return [load(i, src.at[:, j * SLAB:(j + 1) * SLAB], dst.at[j]) for j in range(dst.shape[0])]
+
+    def cols(ref, rows, lo, n):
+        parts = [ref[j, rows] for j in range(lo // SLAB, (lo + n) // SLAB)]
+        return parts[0] if len(parts) == 1 else jnp.concatenate(parts, axis=1)
+
     def rows_of(owner):
         return pl.ds(pl.multiple_of(owner * tb, tb), tb)
 
     def half_of(which):
         return pl.ds(pl.multiple_of(which * half, 128), half)
 
-    def remote(src, dst, send, recv, dev):
-        return pltpu.make_async_remote_copy(src_ref=src, dst_ref=dst, send_sem=send, recv_sem=recv, device_id={'tp': dev}, device_id_type=MESH)
+    def remote(src, dst, recv, dev):
+        return pltpu.make_async_remote_copy(src_ref=src, dst_ref=dst, send_sem=out_sem.at[0], recv_sem=recv, device_id={'tp': dev}, device_id_type=MESH)
 
     def wide(gain, lo, n):
         return jnp.concatenate([gain[i:i + 1] for i in range(lo // HD, (lo + n) // HD)], axis=1)
@@ -86,17 +103,28 @@
         pl.semaphore_signal(barrier, inc=1, device_id={'tp': other}, device_id_type=MESH)
 
     own = rows_of(me)
-    loads = [load(0, x_hbm, xown), load(1, g1_hbm, g1), load(2, g2_hbm, g2), load(12, start_hbm, start_s), load(13, invf_hbm, invf),
-             load(14, x_hbm.at[:, half_of(core)], xh.at[own]),
-             load(3, kc_hbm, kbuf), load(4, vc_hbm, vbuf),
-             load(5, wk_hbm, wk), load(6, wv_hbm, wv), load(7, wq_hbm, wq), load(8, wo_hbm, wo), load(9, wg_hbm, wg),
-             load(10, wu_hbm, wu), load(11, wd_hbm, wd)]
-    (ld_x, ld_g1, ld_g2, ld_start, ld_invf, ld_xh, ld_kc, ld_vc, ld_wk, ld_wv, ld_wq, ld_wo, ld_wg, ld_wu, ld_wd) = loads
-    for item in loads:
+    ld_x = [load(0, x_hbm, xown), load(0, g1_hbm, g1)]
+    ld_small = [load(1, g2_hbm, g2), load(1, start_hbm, start_s), load(1, invf_hbm, invf), load(1, x_hbm.at[:, half_of(core)], xh.at[own])]
+    ld_cache = [load(2, kc_hbm, kbuf), load(2, vc_hbm, vbuf)]
+    ld_wkv = [load(3, wk_hbm, wk), load(3, wv_hbm, wv)]
+    ld_wq = [load(4, wq_hbm, wq)]
+    ld_wo = slabs(5, wo_hbm, wo)
+    ld_gu = slabs(6, wg_hbm, wg) + slabs(6, wu_hbm, wu)
+    n_main = wd.shape[0]
+    wd_slabs = [wd.at[j] if j < n_main else wq.at[pl.ds((j - n_main) * F, F)] for j in range(D // HD)]
+    ld_wd = [load(7, wd_hbm.at[:, j * HD:(j + 1) * HD], wd_slabs[j]) for j in range(D // HD)]
+
+    def wd_cols(lo, n):
+        return jnp.concatenate([wd_slabs[j][...] for j in range(lo // HD, (lo + n) // HD)], axis=1)
+
+    def wait(group):
+        for item in group:
+            item.wait()
+
+    for item in ld_x + ld_small + ld_cache + ld_wkv + ld_wq + ld_wo + ld_gu + ld_wd[:n_main]:
         item.start()
 
-    ld_x.wait()
-    ld_g1.wait()
+    wait(ld_x)
     x32 = xown[...].astype(F32)
     inv = lax.rsqrt(jnp.mean(x32 * x32, axis=-1, keepdims=True) + NORM_EPS)
     nbuf[own] = (x32 * inv * wide(g1[...].astype(F32), 0, D)).astype(BF16)
@@ -104,9 +132,9 @@
     ag_a = []
     for c in range(NAG):
         piece = nbuf.at[own, pl.ds(c * AW, AW)]
-        ag_a.append(remote(piece, piece, aga_s.at[c], aga_r.at[c], across))
+        ag_a.append(remote(piece, piece, aga_r.at[c], across))
         ag_a[c].start()
-    ag_p = remote(nbuf.at[own], nbuf.at[own], agp_s.at[0], agp_r.at[0], partner)
+    ag_p = remote(nbuf.at[own], nbuf.at[own], agp_r.at[0], partner)
     ag_p.start()
 
     row = lax.broadcasted_iota(jnp.int32, (256, 256), 0)
@@ -123,33 +151,30 @@
         lax.fori_loop(lo, hi, body, 0, unroll=min(8, hi - lo))
 
     phase('wait_cache')
-    ld_kc.wait()
-    ld_vc.wait()
+    wait(ld_cache)
     phase('split_cache')
     split(kbuf, vbuf, 0, kbuf.shape[0])
     phase('wait_wkv')
-    ld_wk.wait()
-    ld_wv.wait()
+    wait(ld_wkv)
     ag_f = []
     per_ag = wk.shape[0] // NAG
     for c in range(NAG):
         phase(f'wait_across{c}')
         ag_a[c].wait_recv()
         piece = nbuf.at[rows_of(across), pl.ds(c * AW, AW)]
-        ag_f.append(remote(piece, piece, agf_s.at[c], agf_r.at[c], partner))
+        ag_f.append(remote(piece, piece, agf_r.at[c], partner))
         ag_f[c].start()
         phase(f'split_wkv{c}')
         split(wk, wv, c * per_ag, (c + 1) * per_ag)
 
-    x_sends = [remote(xown.at[:, half_of(core)], xh.at[own], xs_s.at[0], xs_r.at[0], across),
-               remote(xown.at[:, half_of(1 - core)], xh.at[own], xs_s.at[1], xs_r.at[1], diag),
-               remote(xown.at[:, half_of(1 - core)], xh.at[own], xs_s.at[2], xs_r.at[2], partner)]
+    x_sends = [remote(xown.at[:, half_of(core)], xh.at[own], xs_r.at[0], across),
+               remote(xown.at[:, half_of(1 - core)], xh.at[own], xs_r.at[1], diag),
+               remote(xown.at[:, half_of(1 - core)], xh.at[own], xs_r.at[2], partner)]
     for cp in x_sends:
         cp.start()
 
     phase('trig')
-    ld_start.wait()
-    ld_invf.wait()
+    wait(ld_small)
     start = start_s[0]
     lane = lax.broadcasted_iota(jnp.int32, (T, HD), 1)
     tok = lax.broadcasted_iota(jnp.int32, (T, HD), 0)
@@ -170,7 +195,8 @@
         return ref[c * per_ag:(c + 1) * per_ag, g * 128:(g + 1) * 128, :].reshape(AW, HD)
 
     ag_p.wait_recv()
-    ld_wq.wait()
+    wait(ld_wq)
+    ubuf[T:] = jnp.zeros((T, F), BF16)
     kch[...] = jnp.zeros_like(kch)
     vch[...] = jnp.zeros_like(vch)
     for c in range(NAG):
@@ -180,29 +206,20 @@
         rows = nbuf[:, c * AW:(c + 1) * AW]
         for o in range(5):
             if o < 3:
-                w = jnp.concatenate([wq[2 * o, c * AW:(c + 1) * AW], wq[2 * o + 1, c * AW:(c + 1) * AW]], axis=1)
+                w = jnp.concatenate([wq[h * D + c * AW:h * D + (c + 1) * AW] for h in (2 * o, 2 * o + 1)], axis=1)
             else:
                 ref = wk if o == 3 else wv
                 w = jnp.concatenate([split_rows(ref, 0, c), split_rows(ref, 1, c)], axis=1)
             p = dot(rows, w)
             qacc[o] = p if c == 0 else qacc[o] + p
     phase('rope')
+    for item in ld_wd[n_main:]:
+        item.start()
     for g in range(2):
         kch[g, :T] = rope(qacc[3, :, g * HD:(g + 1) * HD]).astype(BF16)
         vch[g, :T] = qacc[4, :, g * HD:(g + 1) * HD].astype(BF16)
     for head in range(6):
         qbuf[head // 3, (head % 3) * T:(head % 3 + 1) * T] = rope(qacc[head // 2, :, (head % 2) * HD:(head % 2 + 1) * HD]).astype(BF16)
-
-    phase('kvout')
-    prow = lax.broadcasted_iota(jnp.int32, (2 * T, HD), 0)
-    pcol = lax.broadcasted_iota(jnp.int32, (2 * T, HD), 1)
-    for src, dst in ((kch, kout), (vch, vout)):
-        mix = sum(dot(jnp.where(prow == 2 * pcol + g, 1.0, 0.0).astype(BF16), src[g]) for g in range(2))
-        dst[...] = mix.astype(BF16)
-    store_k = pltpu.make_async_copy(kout, kn_hbm, st_sem.at[0])
-    store_v = pltpu.make_async_copy(vout, vn_hbm, st_sem.at[1])
-    store_k.start()
-    store_v.start()
 
     phase('attn')
     coef = HD ** -0.5 * float(np.log2(np.e))
@@ -282,31 +299,43 @@
             obuf[:, head * HD:(head + 1) * HD] = acc[g][h * T:(h + 1) * T].astype(BF16)
 
     phase('oproj')
-    ld_wo.wait()
+    wait(ld_wo)
     hop1, hop2, hop3, hop4, hop5 = [], [], [], [], []
+    def out_chunk(c):
+        return [dot(obuf[...], cols(wo, slice(None), i * half + c * HW, HW)) for i in range(2)]
+
+    ready = out_chunk(0)
     for c in range(NCH):
+        now, ready = ready, out_chunk(c + 1) if c + 1 < NCH else None
         for i in range(2):
-            lo = i * half + c * HW
-            part[c, i] = dot(obuf[...], wo[:, lo:lo + HW]).astype(BF16)
-        hop1.append(remote(part.at[c, 1 - core], rx1.at[c], s1.at[c], r1.at[c], partner))
+            part[c, i] = now[i].astype(BF16)
+        hop1.append(remote(part.at[c, 1 - core], rx1.at[c], r1.at[c], partner))
         hop1[c].start()
     phase('hop1')
     for c in range(NCH):
         hop1[c].wait_recv()
         cs[c] = (part[c, core].astype(F32) + rx1[c].astype(F32)).astype(BF16)
-        hop2.append(remote(cs.at[c], rx2.at[c], s2.at[c], r2.at[c], across))
+        hop2.append(remote(cs.at[c], rx2.at[c], r2.at[c], across))
         hop2[c].start()
+
+    phase('kvout')
+    prow = lax.broadcasted_iota(jnp.int32, (2 * T, HD), 0)
+    pcol = lax.broadcasted_iota(jnp.int32, (2 * T, HD), 1)
+    for src, dst in ((kch, kout), (vch, vout)):
+        mix = sum(dot(jnp.where(prow == 2 * pcol + g, 1.0, 0.0).astype(BF16), src[g]) for g in range(2))
+        dst[...] = mix.astype(BF16)
+    store_k = pltpu.make_async_copy(kout, kn_hbm.at[:2 * T], st_sem.at[0])
+    store_v = pltpu.make_async_copy(vout, vn_hbm.at[:2 * T], st_sem.at[0])
+    store_k.start()
+    store_v.start()
 
     phase('hop2')
     for cp in x_sends:
         cp.wait_recv()
-    ld_xh.wait()
-    ld_g2.wait()
     gain2 = g2[...].astype(F32)
     g_top = jnp.maximum(jnp.max(jnp.max(jnp.abs(gain2), axis=1, keepdims=True), axis=0, keepdims=True), 1e-30)
     gain2 = gain2 / g_top
-    ld_wg.wait()
-    ld_wu.wait()
+    wait(ld_gu)
     squares = []
 
     def gate_up(c):
@@ -315,13 +344,13 @@
         lhs = []
         for i in range(2):
             h32 = hbuf[c, i].astype(F32)
-            lhs.append((h32 * wide(gain2, i * half + c * HW, HW)).astype(BF16))
+            lhs.append(jnp.concatenate([(h32 * wide(gain2, i * half + c * HW, HW)).astype(BF16), jnp.zeros((T, HW), BF16)], axis=0))
             for j in range(HW // 128):
                 piece = h32[:, j * 128:(j + 1) * 128]
                 squares.append(piece * piece if not squares else squares.pop() + piece * piece)
         for k, w in enumerate((wg, wu)):
             for lo in range(0, F, 512):
-                p = sum(dot(lhs[i], w[i * half + c * HW:i * half + (c + 1) * HW, lo:lo + 512]) for i in range(2))
+                p = sum(dot_padded(lhs[i], cols(w, slice(i * half + c * HW, i * half + (c + 1) * HW), lo, 512)) for i in range(2))
                 gacc[k, :, lo:lo + 512] = p if c == 0 else gacc[k, :, lo:lo + 512] + p
 
     for c in range(NCH):
@@ -329,7 +358,7 @@
         hop2[c].wait_recv()
         total = cs[c].astype(F32) + rx2[c].astype(F32)
         hbuf[c, core] = (xh[:, c * HW:(c + 1) * HW].astype(F32) + total).astype(BF16)
-        hop3.append(remote(hbuf.at[c, core], hbuf.at[c, core], s3.at[c], r3.at[c], partner))
+        hop3.append(remote(hbuf.at[c, core], hbuf.at[c, core], r3.at[c], partner))
         hop3[c].start()
         if c >= 2:
             gate_up(c - 2)
@@ -341,24 +370,28 @@
     inv2 = inv2 * g_top
     gate = jnp.where(inv2 > 0, gacc[0] * inv2, 0.0)
     up = jnp.where(inv2 > 0, gacc[1] * inv2, 0.0)
-    ubuf[...] = (gate * jax.nn.sigmoid(gate) * up).astype(BF16)
+    ubuf[:T] = (gate * jax.nn.sigmoid(gate) * up).astype(BF16)
 
     phase('down')
-    ld_wd.wait()
+    wait(ld_wd)
     mine = rows_of(chip)
     theirs = rows_of(1 - chip)
 
     def chip_sum(c):
         hop4[c].wait_recv()
         cs2[c] = (part2[c, core, theirs].astype(F32) + rx4[c, theirs].astype(F32)).astype(BF16)
-        hop5.append(remote(cs2.at[c], rx5.at[c], s5.at[c], r5.at[c], across))
+        hop5.append(remote(cs2.at[c], rx5.at[c], r5.at[c], across))
         hop5[c].start()
 
+    def down_chunk(c):
+        return dot_padded(ubuf[...], wd_cols(c * CW, CW))
+
+    ready = down_chunk(0)
     for c in range(NCH2):
-        p = dot(ubuf[...], wd[:, c * CW:(c + 1) * CW]).astype(BF16)
+        p, ready = ready.astype(BF16), down_chunk(c + 1) if c + 1 < NCH2 else None
         for o in range(4):
             part2[c, o % 2, (o // 2) * tb:(o // 2 + 1) * tb] = p[o * tb:(o + 1) * tb]
-        hop4.append(remote(part2.at[c, 1 - core], rx4.at[c], s4.at[c], r4.at[c], partner))
+        hop4.append(remote(part2.at[c, 1 - core], rx4.at[c], r4.at[c], partner))
         hop4[c].start()
         if c >= LAG:
             chip_sum(c - LAG)
@@ -373,7 +406,7 @@
             lo = c * CW + j * HW
             h_own = hbuf[(lo % half) // HW, lo // half, own].astype(F32)
             xout[:, lo:lo + HW] = (h_own + local[:, j * HW:(j + 1) * HW]).astype(BF16)
-    store_x = pltpu.make_async_copy(xout, xo_hbm, st_sem.at[2])
+    store_x = pltpu.make_async_copy(xout, xo_hbm.at[:tb], st_sem.at[0])
     phase('fin')
     store_x.start()
     for cp in ag_a + [ag_p] + ag_f + x_sends + hop1 + hop2 + hop3 + hop4 + hop5:
@@ -385,49 +418,47 @@
 
 
 def cache_kernel(start_ref, kc, vc, kch, vch, xin, kn, vn, xo, kbuf, vbuf, kcb, vcb, xb, in_sem, out_sem):
-    nblk = kc.shape[0]
-    per = kc.shape[1]
+    nblk, per, _ = kc.shape
     rows = nblk * per
-    small = [pltpu.make_async_copy(kch, kcb, in_sem.at[0, nblk]), pltpu.make_async_copy(vch, vcb, in_sem.at[1, nblk]),
-             pltpu.make_async_copy(xin, xb, in_sem.at[2, nblk])]
+    small = [pltpu.make_async_copy(src, dst, in_sem.at[0]) for src, dst in ((kch.at[:kcb.shape[0]], kcb), (vch.at[:vcb.shape[0]], vcb), (xin.at[:xb.shape[0]], xb))]
     for cp in small:
         cp.start()
-    reads = []
+    first = lax.rem(2 * start_ref[0], rows)
+    jrow = lax.broadcasted_iota(jnp.int32, (per, 128), 0)
+    jcol = lax.broadcasted_iota(jnp.int32, (per, 128), 1)
+
+    def touched(b):
+        ahead = lax.rem(b * per - first + rows, rows)
+        return (ahead < 128) | (ahead > rows - per)
+
+    def writes(b, k_src, v_src):
+        return [pltpu.make_async_copy(k_src.at[b], kn.at[b], out_sem.at[0]), pltpu.make_async_copy(v_src.at[b], vn.at[b], out_sem.at[0])]
+
     for b in range(nblk):
-        for i, (src, dst) in enumerate(((kc, kbuf), (vc, vbuf))):
-            cp = pltpu.make_async_copy(src.at[b], dst.at[b], in_sem.at[i, b])
-            cp.start()
-            reads.append(cp)
-    start = start_ref[0]
+        @pl.when(jnp.logical_not(touched(b)))
+        def _():
+            for cp in writes(b, kc, vc):
+                cp.start()
+
     for cp in small:
         cp.wait()
-    xw = pltpu.make_async_copy(xb, xo, out_sem.at[2, 0])
-    xw.start()
-    first = lax.rem(2 * start, rows)
-    writes = [xw]
-    jrow = lax.broadcasted_iota(jnp.int32, (per, 128), 0)
-    jcol = lax.broadcasted_iota(jnp.int32, (per, 128), 1)
+    x_write = pltpu.make_async_copy(xb, xo, out_sem.at[0])
+    x_write.start()
     for b in range(nblk):
-        for i in range(2):
-            reads[2 * b + i].wait()
-        lo = b * per
-        ahead = lax.rem(lo - first + rows, rows)
-        touched = (ahead < 128) | (ahead > rows - per)
-
-        @pl.when(touched)
+        @pl.when(touched(b))
         def _():
-            rel = lax.rem(jrow + lo - first + rows, rows)
+            rel = lax.rem(jrow + b * per - first + rows, rows)
             hot = jnp.where(rel == jcol, 1.0, 0.0).astype(BF16)
             inside = rel < 128
-            kbuf[b] = jnp.where(inside, dot(hot, kcb[...]), kbuf[b].astype(F32)).astype(BF16)
-            vbuf[b] = jnp.where(inside, dot(hot, vcb[...]), vbuf[b].astype(F32)).astype(BF16)
-
-        for i, (src, dst) in enumerate(((kbuf, kn), (vbuf, vn))):
-            cp = pltpu.make_async_copy(src.at[b], dst.at[b], out_sem.at[i, b])
-            cp.start()
-            writes.append(cp)
-    for cp in writes:
-        cp.wait()
+            kbuf[b] = jnp.where(inside, dot(hot, kcb[...]), kc[b].astype(F32)).astype(BF16)
+            vbuf[b] = jnp.where(inside, dot(hot, vcb[...]), vc[b].astype(F32)).astype(BF16)
+            for cp in writes(b, kbuf, vbuf):
+                cp.start()
+
+    x_write.wait()
+    for b in range(nblk):
+        for cp in writes(b, kbuf, vbuf):
+            cp.wait()
 
 
 def solution(mesh):
@@ -457,35 +488,37 @@
         x_out, k_ch, v_ch = pl.pallas_call(
             layer_kernel,
             name='layer',
-            out_shape=(jax.ShapeDtypeStruct((tb, D), BF16), jax.ShapeDtypeStruct((2 * T, HD), BF16), jax.ShapeDtypeStruct((2 * T, HD), BF16)),
+            out_shape=(jax.ShapeDtypeStruct((SPARE // D, D), BF16), jax.ShapeDtypeStruct((SPARE // HD, HD), BF16), jax.ShapeDtypeStruct((SPARE // HD, HD), BF16)),
             in_specs=[any_spec] * 14,
             out_specs=(any_spec,) * 3,
             scratch_shapes=[
                 pltpu.SMEM((1,), jnp.int32), vmem((1, HD), F32),
                 vmem((tb, D), BF16), vmem((T, D // 2), BF16), vmem((T, D), BF16), vmem((D // HD, HD), BF16), vmem((D // HD, HD), BF16),
                 vmem((blocks, 256, HD), BF16), vmem((blocks, 256, HD), BF16),
-                vmem((qh, D, HD), BF16), vmem((D // 128, 256, HD), BF16), vmem((D // 128, 256, HD), BF16),
-                vmem((qh * HD, D), BF16), vmem((D, F), BF16), vmem((D, F), BF16), vmem((F, D), BF16),
+                vmem((qh * D, HD), BF16), vmem((D // 128, 256, HD), BF16), vmem((D // 128, 256, HD), BF16),
+                vmem((D // SLAB, qh * HD, SLAB), BF16), vmem((F // SLAB, D, SLAB), BF16), vmem((F // SLAB, D, SLAB), BF16), vmem((D // HD - qh * D // F, F, HD), BF16),
                 vmem((5, T, 256), F32), vmem((8, window), jnp.int32),
                 vmem((2, window // KB, 3 * T, KB), F32), vmem((2, 3 * T, HD), BF16), vmem((2, 128, HD), BF16), vmem((2, 128, HD), BF16),
                 vmem((T, qh * HD), BF16),
                 vmem((NCH, 2, T, HW), BF16), vmem((NCH, T, HW), BF16), vmem((NCH, T, HW), BF16), vmem((NCH, T, HW), BF16),
-                vmem((NCH, 2, T, HW), BF16), vmem((2, T, F), F32), vmem((T, F), BF16),
+                vmem((NCH, 2, T, HW), BF16), vmem((2, T, F), F32), vmem((2 * T, F), BF16),
                 vmem((NCH2, 2, 2 * tb, CW), BF16), vmem((NCH2, 2 * tb, CW), BF16), vmem((NCH2, tb, CW), BF16), vmem((NCH2, tb, CW), BF16),
                 vmem((tb, D), BF16), vmem((2 * T, HD), BF16), vmem((2 * T, HD), BF16),
-                dma((15,)), dma((3,)), dma((1,)), dma((1,))] + [dma((NAG,))] * 4 + [dma((3,))] * 2 + [dma((NCH,))] * 6 + [dma((NCH2,))] * 4,
-            compiler_params=pltpu.CompilerParams(collective_id=0, has_side_effects=True, vmem_limit_bytes=67043328),
-        )(start_pos, invf, x_in.reshape(tb, D), attn_gain.reshape(D // HD, HD), mlp_gain.reshape(D // HD, HD), kc, vc, w_query.transpose(1, 0, 2), wk, wv,
+                dma((8,)), dma((1,)), dma((1,)), dma((1,))] + [dma((NAG,))] * 2 + [dma((3,))] + [dma((NCH,))] * 3 + [dma((NCH2,))] * 2,
+            compiler_params=pltpu.CompilerParams(collective_id=0, has_side_effects=True, vmem_limit_bytes=LAYER_VMEM),
+            cost_estimate=pl.CostEstimate(flops=2 * 64 * 25 * 10**6, bytes_accessed=80 * 10**6, transcendentals=3 * 10**6),
+        )(start_pos, invf, x_in.reshape(tb, D), attn_gain.reshape(D // HD, HD), mlp_gain.reshape(D // HD, HD), kc, vc, w_query.transpose(1, 0, 2).reshape(qh * D, HD), wk, wv,
           w_out.reshape(qh * HD, D), w_gate, w_up, w_down)
-        nblk = 8
+        nblk = 16
         per = 2 * window // nblk
         k_new, v_new, x_fin = pl.pallas_call(
             cache_kernel,
             name='cache',
             out_shape=(jax.ShapeDtypeStruct((nblk, per, HD), BF16),) * 2 + (jax.ShapeDtypeStruct((tb, D), BF16),),
-            in_specs=[pl.BlockSpec(memory_space=pltpu.SMEM)] + [any_spec] * 5,
+            in_specs=[pl.BlockSpec(memory_space=pltpu.SMEM)] + [pl.BlockSpec(memory_space=pltpu.VMEM)] * 2 + [pl.BlockSpec(memory_space=pltpu.HBM)] * 3,
             out_specs=(any_spec,) * 3,
-            scratch_shapes=[vmem((nblk, per, HD), BF16)] * 2 + [vmem((2 * T, HD), BF16)] * 2 + [vmem((tb, D), BF16), dma((3, nblk + 1)), dma((3, nblk))],
+            scratch_shapes=[vmem((nblk, per, HD), BF16)] * 2 + [vmem((2 * T, HD), BF16)] * 2 + [vmem((tb, D), BF16), dma((1,)), dma((1,))],
+            compiler_params=pltpu.CompilerParams(vmem_limit_bytes=CACHE_VMEM),
         )(start_pos, k_cache.reshape(nblk, per, HD), v_cache.reshape(nblk, per, HD), k_ch, v_ch, x_out)
         return x_fin.reshape(x_in.shape), k_new.reshape(k_cache.shape), v_new.reshape(v_cache.shape)
 

time: 37.3 us -> 33.7 us (0.903)
  Pallas kernels: 36 us -> 32.1 us
    pallas_call x1, Pallas kernels: 31.9 us -> 29.9 us  [local_layer(): pl.pallas_call(layer_kernel, name='layer', out_shape=(jax.ShapeDtypeStruc...]
    pallas_call x1, Pallas kernels: 4.06 us -> 2.14 us  [local_layer(): pl.pallas_call(cache_kernel, name='cache', out_shape=(jax.ShapeDtypeStruc...]
where the time goes in v3:
time: 33.7 us; the launch traced here: 33.5 us
  Pallas kernels  32.1 us (95%)
  between operations  1.48 us (4%)
    pallas_call x1, Pallas kernels, local_layer(): pl.pallas_call(layer_kernel, name='layer', out_shape=(jax.ShapeDtypeStruc...  29.9 us
    pallas_call x1, Pallas kernels, local_layer(): pl.pallas_call(cache_kernel, name='cache', out_shape=(jax.ShapeDtypeStruc...  2.14 us

profile of v3, /device:TPU:0, one launch (start us, length us, event | category | flops | bytes accessed | tf_op | source)
XLA Modules:
  0.0 33.5 jit_solution(6987435885063280617)
XLA Ops:
  1.3 0.0 copy-start
  1.3 0.0 copy-start.1
  1.3 29.9 %layer.1 = (bf16[8192,3072]{1,0:T(8,128)(2,1)}, bf16[196608,128]{1,0:T(8,128)(2,1)}, bf16[196608,128]{1,0:T(8,128)(2,1)}) custom-call(s32[1]{0:T(128)S(6)} %copy.17.start_hbm.start_ref, f32[1,128]{1,0:T(1,128)} %constant.2.clone.invf_hbm, bf16[16,3072]{1,0:T(8,128)(2,1)} %bitcast.24, bf16[24,128]{1,0:T(8,128)(2,1)} %bitcast.25, bf16[24,128]{1,0:T(8,128)(2,1)} %bitcast.26, ...), custom_call_target="tpu_custom_call" | custom-call | flops 3200000000 | bytes 80000000 | tf_op jit(solution)/shard_map/layer/pallas_call | solution.py:488
  31.2 0.0 copy-done
  31.2 0.0 copy-done.1
  31.2 2.1 %cache.1 = (bf16[16,512,128]{2,1,0:T(8,128)(2,1)}, bf16[16,512,128]{2,1,0:T(8,128)(2,1)}, bf16[16,3072]{1,0:T(8,128)(2,1)}) custom-call(s32[1]{0:T(128)S(6)} %copy.17.start_hbm.start_ref, bf16[16,512,128]{2,1,0:T(8,128)(2,1)S(1)} %bitcast.17, bf16[16,512,128]{2,1,0:T(8,128)(2,1)S(1)} %bitcast.19, bf16[196608,128]{1,0:T(8,128)(2,1)} %get-tuple-element.9.kch, ...), custom_call_target="tpu_custom_call" | custom-call | tf_op jit(solution)/shard_map/cache/pallas_call | solution.py:514
Async XLA Ops:
  1.3 29.9 %copy-start = (bf16[1,4096,2,128]{3,2,1,0:T(2,128)(2,1)S(1)}, bf16[1,4096,2,128]{3,2,1,0:T(2,128)(2,1)}, u32[]{:S(2)}) copy-start(bf16[1,4096,2,128]{3,2,1,0:T(2,128)(2,1)} %param.16) | copy-start | bytes 6291460
  1.3 29.9 %copy-start.1 = (bf16[1,4096,2,128]{3,2,1,0:T(2,128)(2,1)S(1)}, bf16[1,4096,2,128]{3,2,1,0:T(2,128)(2,1)}, u32[]{:S(2)}) copy-start(bf16[1,4096,2,128]{3,2,1,0:T(2,128)(2,1)} %param.17) | copy-start | bytes 6291460

commit v4 on v3

--- a/solution.py
+++ b/solution.py
@@ -14,13 +14,17 @@
 BF16 = jnp.bfloat16
 F32 = jnp.float32
 HD = 128
-NCH = 6
-NCH2 = 6
+OUT_W = (256, 256, 256, 256, 256, 256)
+OUT_LO = tuple(sum(OUT_W[:i]) for i in range(len(OUT_W)))
+NCH = len(OUT_W)
+OUT_GROUPS = ((0,), (1, 2), (3, 4, 5))
+DOWN = (0, 1024, 2048, 2560, 3072)
 NAG = 4
 LAG = 2
+GLAG = 2
 KB = 512
 SLAB = 256
-LAYER_VMEM = 62 * 10**6
+LAYER_VMEM = 62600000
 CACHE_VMEM = 24 * 10**6
 SPARE = 3 * 2**23
 
@@ -58,13 +62,11 @@
                  xo_hbm, kn_hbm, vn_hbm,
                  start_s, invf, xown, xh, nbuf, g1, g2, kbuf, vbuf, wq, wk, wv, wo, wg, wu, wd,
                  qacc, offb, sbuf, qbuf, kch, vch, obuf, part, rx1, cs, rx2, hbuf, gacc, ubuf, part2, rx4, cs2, rx5, xout, kout, vout,
-                 ld_sem, st_sem, out_sem, agp_r, aga_r, agf_r, xs_r, r1, r2, r3, r4, r5):
+                 ld_sem, st_sem, out_sem, agp_r, aga_r, xs_r, r1, r2, r3, r5):
     phase = Phases()
     phase('entry')
     T, D = nbuf.shape
     half = D // 2
-    HW = half // NCH
-    CW = D // NCH2
     AW = D // NAG
     tb = T // 4
     window = kbuf.shape[0] * 128
@@ -83,8 +85,11 @@
         return [load(i, src.at[:, j * SLAB:(j + 1) * SLAB], dst.at[j]) for j in range(dst.shape[0])]
 
     def cols(ref, rows, lo, n):
-        parts = [ref[j, rows] for j in range(lo // SLAB, (lo + n) // SLAB)]
+        parts = [ref[j * HD // SLAB, rows, j * HD % SLAB:j * HD % SLAB + HD] for j in range(lo // HD, (lo + n) // HD)]
         return parts[0] if len(parts) == 1 else jnp.concatenate(parts, axis=1)
+
+    def span(c):
+        return slice(OUT_LO[c], OUT_LO[c] + OUT_W[c])
 
     def rows_of(owner):
         return pl.ds(pl.multiple_of(owner * tb, tb), tb)
@@ -136,42 +141,6 @@
         ag_a[c].start()
     ag_p = remote(nbuf.at[own], nbuf.at[own], agp_r.at[0], partner)
     ag_p.start()
-
-    row = lax.broadcasted_iota(jnp.int32, (256, 256), 0)
-    col = lax.broadcasted_iota(jnp.int32, (256, 256), 1)
-    pick = jnp.where(col == 2 * lax.rem(row, 128) + lax.div(row, 128), 1.0, 0.0).astype(BF16)
-
-    def split(a_ref, b_ref, lo, hi):
-        def body(b, carry):
-            both = jnp.concatenate([a_ref[b], b_ref[b]], axis=1)
-            sep = dot(pick, both).astype(BF16)
-            a_ref[b] = sep[:, :128]
-            b_ref[b] = sep[:, 128:]
-            return carry
-        lax.fori_loop(lo, hi, body, 0, unroll=min(8, hi - lo))
-
-    phase('wait_cache')
-    wait(ld_cache)
-    phase('split_cache')
-    split(kbuf, vbuf, 0, kbuf.shape[0])
-    phase('wait_wkv')
-    wait(ld_wkv)
-    ag_f = []
-    per_ag = wk.shape[0] // NAG
-    for c in range(NAG):
-        phase(f'wait_across{c}')
-        ag_a[c].wait_recv()
-        piece = nbuf.at[rows_of(across), pl.ds(c * AW, AW)]
-        ag_f.append(remote(piece, piece, agf_r.at[c], partner))
-        ag_f[c].start()
-        phase(f'split_wkv{c}')
-        split(wk, wv, c * per_ag, (c + 1) * per_ag)
-
-    x_sends = [remote(xown.at[:, half_of(core)], xh.at[own], xs_r.at[0], across),
-               remote(xown.at[:, half_of(1 - core)], xh.at[own], xs_r.at[1], diag),
-               remote(xown.at[:, half_of(1 - core)], xh.at[own], xs_r.at[2], partner)]
-    for cp in x_sends:
-        cp.start()
 
     phase('trig')
     wait(ld_small)
@@ -191,8 +160,44 @@
         swapped = jnp.where(even, pltpu.roll(h, HD - 1, 1), pltpu.roll(h, 1, 1))
         return h * cos_t + swapped * sin_t
 
+    row = lax.broadcasted_iota(jnp.int32, (256, 256), 0)
+    col = lax.broadcasted_iota(jnp.int32, (256, 256), 1)
+    pick = jnp.where(col == 2 * lax.rem(row, 128) + lax.div(row, 128), 1.0, 0.0).astype(BF16)
+
+    def split(a_ref, b_ref, lo, hi):
+        def body(b, carry):
+            both = jnp.concatenate([a_ref[b], b_ref[b]], axis=1)
+            sep = dot(pick, both).astype(BF16)
+            a_ref[b] = sep[:, :128]
+            b_ref[b] = sep[:, 128:]
+            return carry
+        lax.fori_loop(lo, hi, body, 0, unroll=12 if (hi - lo) % 12 == 0 else 16)
+
+    phase('wait_cache')
+    wait(ld_cache)
+    phase('split_cache')
+    split(kbuf, vbuf, 0, kbuf.shape[0])
+    phase('wait_wkv')
+    wait(ld_wkv)
+    ag_f = []
+
+    def relay(c):
+        ag_a[c].wait_recv()
+        piece = nbuf.at[rows_of(across), pl.ds(c * AW, AW)]
+        ag_f.append(remote(piece, piece, r3.at[c], partner))
+        ag_f[c].start()
+
+    phase('split_wkv')
+    split(wk, wv, 0, wk.shape[0])
+    for c in range(NAG):
+        phase(f'wait_across{c}')
+        relay(c)
+
+    QW = AW
+    per_q = QW // 128
+
     def split_rows(ref, g, c):
-        return ref[c * per_ag:(c + 1) * per_ag, g * 128:(g + 1) * 128, :].reshape(AW, HD)
+        return ref[c * per_q:(c + 1) * per_q, g * 128:(g + 1) * 128, :].reshape(QW, HD)
 
     ag_p.wait_recv()
     wait(ld_wq)
@@ -203,16 +208,22 @@
         phase(f'wait_fwd{c}')
         ag_f[c].wait_recv()
         phase(f'qkv{c}')
-        rows = nbuf[:, c * AW:(c + 1) * AW]
+        rows = nbuf[:, c * QW:(c + 1) * QW]
         for o in range(5):
             if o < 3:
-                w = jnp.concatenate([wq[h * D + c * AW:h * D + (c + 1) * AW] for h in (2 * o, 2 * o + 1)], axis=1)
+                w = jnp.concatenate([wq[h * D + c * QW:h * D + (c + 1) * QW] for h in (2 * o, 2 * o + 1)], axis=1)
             else:
                 ref = wk if o == 3 else wv
                 w = jnp.concatenate([split_rows(ref, 0, c), split_rows(ref, 1, c)], axis=1)
             p = dot(rows, w)
             qacc[o] = p if c == 0 else qacc[o] + p
     phase('rope')
+    x_sends = [remote(xown.at[:, half_of(core)], xh.at[own], xs_r.at[0], across),
+               remote(xown.at[:, half_of(1 - core)], xh.at[own], xs_r.at[1], diag),
+               remote(xown.at[:, half_of(1 - core)], xh.at[own], xs_r.at[2], partner)]
+    for cp in x_sends:
+        cp.start()
+
     for item in ld_wd[n_main:]:
         item.start()
     for g in range(2):
@@ -302,20 +313,20 @@
     wait(ld_wo)
     hop1, hop2, hop3, hop4, hop5 = [], [], [], [], []
     def out_chunk(c):
-        return [dot(obuf[...], cols(wo, slice(None), i * half + c * HW, HW)) for i in range(2)]
-
-    ready = out_chunk(0)
-    for c in range(NCH):
-        now, ready = ready, out_chunk(c + 1) if c + 1 < NCH else None
-        for i in range(2):
-            part[c, i] = now[i].astype(BF16)
-        hop1.append(remote(part.at[c, 1 - core], rx1.at[c], r1.at[c], partner))
-        hop1[c].start()
+        return [dot(obuf[...], cols(wo, slice(None), i * half + OUT_LO[c], OUT_W[c])) for i in range(2)]
+
+    for group in OUT_GROUPS:
+        for c in group:
+            for i, p in enumerate(out_chunk(c)):
+                part[i, :, span(c)] = p.astype(BF16)
+        for c in group:
+            hop1.append(remote(part.at[1 - core, :, span(c)], rx1.at[:, span(c)], r1.at[c], partner))
+            hop1[c].start()
     phase('hop1')
     for c in range(NCH):
         hop1[c].wait_recv()
-        cs[c] = (part[c, core].astype(F32) + rx1[c].astype(F32)).astype(BF16)
-        hop2.append(remote(cs.at[c], rx2.at[c], r2.at[c], across))
+        cs[:, span(c)] = (part[core, :, span(c)].astype(F32) + rx1[:, span(c)].astype(F32)).astype(BF16)
+        hop2.append(remote(cs.at[:, span(c)], rx2.at[:, span(c)], r2.at[c], across))
         hop2[c].start()
 
     phase('kvout')
@@ -341,28 +352,31 @@
     def gate_up(c):
         hop3[c].wait_recv()
         phase(f'gateup{c}')
+        lo, w = OUT_LO[c], OUT_W[c]
         lhs = []
         for i in range(2):
-            h32 = hbuf[c, i].astype(F32)
-            lhs.append(jnp.concatenate([(h32 * wide(gain2, i * half + c * HW, HW)).astype(BF16), jnp.zeros((T, HW), BF16)], axis=0))
-            for j in range(HW // 128):
+            h32 = hbuf[i, :, span(c)].astype(F32)
+            lhs.append((h32 * wide(gain2, i * half + lo, w)).astype(BF16))
+            for j in range(w // 128):
                 piece = h32[:, j * 128:(j + 1) * 128]
                 squares.append(piece * piece if not squares else squares.pop() + piece * piece)
-        for k, w in enumerate((wg, wu)):
-            for lo in range(0, F, 512):
-                p = sum(dot_padded(lhs[i], cols(w, slice(i * half + c * HW, i * half + (c + 1) * HW), lo, 512)) for i in range(2))
-                gacc[k, :, lo:lo + 512] = p if c == 0 else gacc[k, :, lo:lo + 512] + p
+        lhs = jnp.concatenate([jnp.concatenate(lhs, axis=1), jnp.zeros((T, 2 * w), BF16)], axis=0)
+        for k, ref in enumerate((wg, wu)):
+            for n in range(0, F, 512):
+                rhs = jnp.concatenate([cols(ref, slice(i * half + lo, i * half + lo + w), n, 512) for i in range(2)], axis=0)
+                p = dot_padded(lhs, rhs)
+                gacc[k, :, n:n + 512] = p if c == 0 else gacc[k, :, n:n + 512] + p
 
     for c in range(NCH):
         phase(f'hop2_{c}')
         hop2[c].wait_recv()
-        total = cs[c].astype(F32) + rx2[c].astype(F32)
-        hbuf[c, core] = (xh[:, c * HW:(c + 1) * HW].astype(F32) + total).astype(BF16)
-        hop3.append(remote(hbuf.at[c, core], hbuf.at[c, core], r3.at[c], partner))
+        total = cs[:, span(c)].astype(F32) + rx2[:, span(c)].astype(F32)
+        hbuf[core, :, span(c)] = (xh[:, span(c)].astype(F32) + total).astype(BF16)
+        hop3.append(remote(hbuf.at[core, :, span(c)], hbuf.at[core, :, span(c)], r3.at[c], partner))
         hop3[c].start()
-        if c >= 2:
-            gate_up(c - 2)
-    for c in range(NCH - 2, NCH):
+        if c >= GLAG:
+            gate_up(c - GLAG)
+    for c in range(NCH - GLAG, NCH):
         phase(f'hop3_{c}')
         gate_up(c)
     phase('act')
@@ -377,35 +391,35 @@
     mine = rows_of(chip)
     theirs = rows_of(1 - chip)
 
+    n_down = len(DOWN) - 1
+
     def chip_sum(c):
         hop4[c].wait_recv()
-        cs2[c] = (part2[c, core, theirs].astype(F32) + rx4[c, theirs].astype(F32)).astype(BF16)
-        hop5.append(remote(cs2.at[c], rx5.at[c], r5.at[c], across))
+        at = slice(DOWN[c], DOWN[c + 1])
+        cs2[:, at] = (part2[core, theirs, at].astype(F32) + rx4[theirs, at].astype(F32)).astype(BF16)
+        hop5.append(remote(cs2.at[:, at], rx5.at[:, at], r5.at[c], across))
         hop5[c].start()
 
-    def down_chunk(c):
-        return dot_padded(ubuf[...], wd_cols(c * CW, CW))
-
-    ready = down_chunk(0)
-    for c in range(NCH2):
-        p, ready = ready.astype(BF16), down_chunk(c + 1) if c + 1 < NCH2 else None
+    for c in range(n_down):
+        lo, hi = DOWN[c], DOWN[c + 1]
+        p = dot_padded(ubuf[...], wd_cols(lo, hi - lo)).astype(BF16)
         for o in range(4):
-            part2[c, o % 2, (o // 2) * tb:(o // 2 + 1) * tb] = p[o * tb:(o + 1) * tb]
-        hop4.append(remote(part2.at[c, 1 - core], rx4.at[c], r4.at[c], partner))
+            part2[o % 2, (o // 2) * tb:(o // 2 + 1) * tb, lo:hi] = p[o * tb:(o + 1) * tb]
+        hop4.append(remote(part2.at[1 - core, :, lo:hi], rx4.at[:, lo:hi], r1.at[c], partner))
         hop4[c].start()
         if c >= LAG:
             chip_sum(c - LAG)
     phase('hop4')
-    for c in range(NCH2 - LAG, NCH2):
+    for c in range(n_down - LAG, n_down):
         chip_sum(c)
     phase('hop5')
-    for c in range(NCH2):
+    for c in range(n_down):
         hop5[c].wait_recv()
-        local = part2[c, core, mine].astype(F32) + rx4[c, mine].astype(F32) + rx5[c].astype(F32)
-        for j in range(CW // HW):
-            lo = c * CW + j * HW
-            h_own = hbuf[(lo % half) // HW, lo // half, own].astype(F32)
-            xout[:, lo:lo + HW] = (h_own + local[:, j * HW:(j + 1) * HW]).astype(BF16)
+        for lo in range(DOWN[c], DOWN[c + 1], SLAB):
+            at = slice(lo, lo + SLAB)
+            h_own = hbuf[lo // half, own, lo % half:lo % half + SLAB].astype(F32)
+            local = part2[core, mine, at].astype(F32) + rx4[mine, at].astype(F32) + rx5[:, at].astype(F32)
+            xout[:, at] = (h_own + local).astype(BF16)
     store_x = pltpu.make_async_copy(xout, xo_hbm.at[:tb], st_sem.at[0])
     phase('fin')
     store_x.start()
@@ -473,8 +487,6 @@
         T = 4 * tb
         window = k_cache.shape[1]
         F = w_gate.shape[1]
-        HW = D // 2 // NCH
-        CW = D // NCH2
         qh = w_query.shape[1]
         invf = jnp.asarray(np.repeat(ROPE_BASE ** (-np.arange(0, HD, 2) / HD), 2).astype(np.float32)[None])
         blocks = window // 128
@@ -500,11 +512,11 @@
                 vmem((5, T, 256), F32), vmem((8, window), jnp.int32),
                 vmem((2, window // KB, 3 * T, KB), F32), vmem((2, 3 * T, HD), BF16), vmem((2, 128, HD), BF16), vmem((2, 128, HD), BF16),
                 vmem((T, qh * HD), BF16),
-                vmem((NCH, 2, T, HW), BF16), vmem((NCH, T, HW), BF16), vmem((NCH, T, HW), BF16), vmem((NCH, T, HW), BF16),
-                vmem((NCH, 2, T, HW), BF16), vmem((2, T, F), F32), vmem((2 * T, F), BF16),
-                vmem((NCH2, 2, 2 * tb, CW), BF16), vmem((NCH2, 2 * tb, CW), BF16), vmem((NCH2, tb, CW), BF16), vmem((NCH2, tb, CW), BF16),
+                vmem((2, T, D // 2), BF16), vmem((T, D // 2), BF16), vmem((T, D // 2), BF16), vmem((T, D // 2), BF16),
+                vmem((2, T, D // 2), BF16), vmem((2, T, F), F32), vmem((2 * T, F), BF16),
+                vmem((2, 2 * tb, D), BF16), vmem((2 * tb, D), BF16), vmem((tb, D), BF16), vmem((tb, D), BF16),
                 vmem((tb, D), BF16), vmem((2 * T, HD), BF16), vmem((2 * T, HD), BF16),
-                dma((8,)), dma((1,)), dma((1,)), dma((1,))] + [dma((NAG,))] * 2 + [dma((3,))] + [dma((NCH,))] * 3 + [dma((NCH2,))] * 2,
+                dma((8,)), dma((1,)), dma((1,)), dma((1,))] + [dma((NAG,)), dma((3,))] + [dma((NCH,))] * 3 + [dma((len(DOWN) - 1,))],
             compiler_params=pltpu.CompilerParams(collective_id=0, has_side_effects=True, vmem_limit_bytes=LAYER_VMEM),
             cost_estimate=pl.CostEstimate(flops=2 * 64 * 25 * 10**6, bytes_accessed=80 * 10**6, transcendentals=3 * 10**6),
         )(start_pos, invf, x_in.reshape(tb, D), attn_gain.reshape(D // HD, HD), mlp_gain.reshape(D // HD, HD), kc, vc, w_query.transpose(1, 0, 2).reshape(qh * D, HD), wk, wv,

time: 33.7 us -> 32.9 us (0.976)
  Pallas kernels: 32.1 us -> 31.3 us
    pallas_call x1, Pallas kernels: 29.9 us -> 29.1 us  [local_layer(): pl.pallas_call(layer_kernel, name='layer', out_shape=(jax.ShapeDtypeStruc...]
where the time goes in v4:
time: 32.9 us; the launch traced here: 32.6 us
  Pallas kernels  31.3 us (95%)
  between operations  1.32 us (4%)
    pallas_call x1, Pallas kernels, local_layer(): pl.pallas_call(layer_kernel, name='layer', out_shape=(jax.ShapeDtypeStruc...  29.1 us
    pallas_call x1, Pallas kernels, local_layer(): pl.pallas_call(cache_kernel, name='cache', out_shape=(jax.ShapeDtypeStruc...  2.14 us

profile of v4, /device:TPU:0, one launch (start us, length us, event | category | flops | bytes accessed | tf_op | source)
XLA Modules:
  0.0 32.6 jit_solution(4011197148373221734)
XLA Ops:
  1.3 0.0 copy-start
  1.3 0.0 copy-start.1
  1.3 29.1 %layer.1 = (bf16[8192,3072]{1,0:T(8,128)(2,1)}, bf16[196608,128]{1,0:T(8,128)(2,1)}, bf16[196608,128]{1,0:T(8,128)(2,1)}) custom-call(s32[1]{0:T(128)S(6)} %copy.17.start_hbm.start_ref, f32[1,128]{1,0:T(1,128)} %constant.2.clone.invf_hbm, bf16[16,3072]{1,0:T(8,128)(2,1)} %bitcast.24, bf16[24,128]{1,0:T(8,128)(2,1)} %bitcast.25, bf16[24,128]{1,0:T(8,128)(2,1)} %bitcast.26, ...), custom_call_target="tpu_custom_call" | custom-call | flops 3200000000 | bytes 80000000 | tf_op jit(solution)/shard_map/layer/pallas_call | solution.py:500
  30.4 0.0 copy-done
  30.4 0.0 copy-done.1
  30.4 2.1 %cache.1 = (bf16[16,512,128]{2,1,0:T(8,128)(2,1)}, bf16[16,512,128]{2,1,0:T(8,128)(2,1)}, bf16[16,3072]{1,0:T(8,128)(2,1)}) custom-call(s32[1]{0:T(128)S(6)} %copy.17.start_hbm.start_ref, bf16[16,512,128]{2,1,0:T(8,128)(2,1)S(1)} %bitcast.17, bf16[16,512,128]{2,1,0:T(8,128)(2,1)S(1)} %bitcast.19, bf16[196608,128]{1,0:T(8,128)(2,1)} %get-tuple-element.9.kch, ...), custom_call_target="tpu_custom_call" | custom-call | tf_op jit(solution)/shard_map/cache/pallas_call | solution.py:526
Async XLA Ops:
  1.3 29.1 %copy-start = (bf16[1,4096,2,128]{3,2,1,0:T(2,128)(2,1)S(1)}, bf16[1,4096,2,128]{3,2,1,0:T(2,128)(2,1)}, u32[]{:S(2)}) copy-start(bf16[1,4096,2,128]{3,2,1,0:T(2,128)(2,1)} %param.16) | copy-start | bytes 6291460
  1.3 29.1 %copy-start.1 = (bf16[1,4096,2,128]{3,2,1,0:T(2,128)(2,1)S(1)}, bf16[1,4096,2,128]{3,2,1,0:T(2,128)(2,1)}, u32[]{:S(2)}) copy-start(bf16[1,4096,2,128]{3,2,1,0:T(2,128)(2,1)} %param.17) | copy-start | bytes 6291460

commit v5 on v4

--- a/solution.py
+++ b/solution.py
@@ -22,6 +22,8 @@
 NAG = 4
 LAG = 2
 GLAG = 2
+PADQ = True
+PVN = 4
 KB = 512
 SLAB = 256
 LAYER_VMEM = 62600000
@@ -193,6 +195,12 @@
         phase(f'wait_across{c}')
         relay(c)
 
+    x_sends = [remote(xown.at[:, half_of(core)], xh.at[own], xs_r.at[0], across),
+               remote(xown.at[:, half_of(1 - core)], xh.at[own], xs_r.at[1], diag),
+               remote(xown.at[:, half_of(1 - core)], xh.at[own], xs_r.at[2], partner)]
+    for cp in x_sends:
+        cp.start()
+
     QW = AW
     per_q = QW // 128
 
@@ -209,23 +217,14 @@
         ag_f[c].wait_recv()
         phase(f'qkv{c}')
         rows = nbuf[:, c * QW:(c + 1) * QW]
+        w = [wq[h * D + c * QW:h * D + (c + 1) * QW] for h in range(6)]
+        w += [split_rows(ref, g, c) for ref in (wk, wv) for g in range(2)]
+        p = dot_padded(jnp.concatenate([rows, jnp.zeros_like(rows)], axis=0), jnp.concatenate(w, axis=1)) if PADQ else dot(rows, jnp.concatenate(w, axis=1))
         for o in range(5):
-            if o < 3:
-                w = jnp.concatenate([wq[h * D + c * QW:h * D + (c + 1) * QW] for h in (2 * o, 2 * o + 1)], axis=1)
-            else:
-                ref = wk if o == 3 else wv
-                w = jnp.concatenate([split_rows(ref, 0, c), split_rows(ref, 1, c)], axis=1)
-            p = dot(rows, w)
-            qacc[o] = p if c == 0 else qacc[o] + p
+            q = p[:, o * 256:(o + 1) * 256]
+            qacc[o] = q if c == 0 else qacc[o] + q
     phase('rope')
-    x_sends = [remote(xown.at[:, half_of(core)], xh.at[own], xs_r.at[0], across),
-               remote(xown.at[:, half_of(1 - core)], xh.at[own], xs_r.at[1], diag),
-               remote(xown.at[:, half_of(1 - core)], xh.at[own], xs_r.at[2], partner)]
-    for cp in x_sends:
-        cp.start()
-
-    for item in ld_wd[n_main:]:
-        item.start()
+
     for g in range(2):
         kch[g, :T] = rope(qacc[3, :, g * HD:(g + 1) * HD]).astype(BF16)
         vch[g, :T] = qacc[4, :, g * HD:(g + 1) * HD].astype(BF16)
@@ -275,15 +274,21 @@
         for j in range(nb):
             mass[g][h] = mass[g][h] + e[:, j * 128:(j + 1) * 128]
 
+    parts = [[], []]
+
     def weigh_chunk(g):
         for h in range(3):
             scale[g][h] = 1.0 / jnp.sum(mass[g][h], axis=1, keepdims=True)
-        p = jnp.concatenate([(e_c[g][h] * scale[g][h]).astype(BF16) for h in range(3)], axis=0)
-        acc[g] = dot(p, vch[g])
+        parts[g].append(jnp.concatenate([(e_c[g][h] * scale[g][h]).astype(BF16) for h in range(3)], axis=0))
 
     def weigh(g, i):
-        p = jnp.concatenate([(sbuf[g, i, h * T:(h + 1) * T] * scale[g][h]).astype(BF16) for h in range(3)], axis=0)
-        acc[g] = acc[g] + dot(p, blocks(vbuf, g, i))
+        parts[g].append(jnp.concatenate([(sbuf[g, i, h * T:(h + 1) * T] * scale[g][h]).astype(BF16) for h in range(3)], axis=0))
+        if i == nblk - 1:
+            acc[g] = dot(parts[g][0], vch[g])
+            n = PVN
+            for k in range(0, nblk, n):
+                p = jnp.concatenate(parts[g][1 + k:1 + k + n], axis=1)
+                acc[g] = acc[g] + dot(p, jnp.concatenate([blocks(vbuf, g, j) for j in range(k, k + n)], axis=0))
 
     order = [(h, i) for h in range(3) for i in range(nblk)]
     score_chunk(0)
@@ -330,6 +335,8 @@
         hop2[c].start()
 
     phase('kvout')
+    for item in ld_wd[n_main:]:
+        item.start()
     prow = lax.broadcasted_iota(jnp.int32, (2 * T, HD), 0)
     pcol = lax.broadcasted_iota(jnp.int32, (2 * T, HD), 1)
     for src, dst in ((kch, kout), (vch, vout)):
@@ -361,11 +368,22 @@
                 piece = h32[:, j * 128:(j + 1) * 128]
                 squares.append(piece * piece if not squares else squares.pop() + piece * piece)
         lhs = jnp.concatenate([jnp.concatenate(lhs, axis=1), jnp.zeros((T, 2 * w), BF16)], axis=0)
-        for k, ref in enumerate((wg, wu)):
-            for n in range(0, F, 512):
+        last = c == NCH - 1
+        if last:
+            inv2 = lax.rsqrt(jnp.sum(squares[0], axis=-1, keepdims=True) / D + NORM_EPS)
+            inv2 = inv2 * g_top
+        for n in range(0, F, 512):
+            both = []
+            for k, ref in enumerate((wg, wu)):
                 rhs = jnp.concatenate([cols(ref, slice(i * half + lo, i * half + lo + w), n, 512) for i in range(2)], axis=0)
                 p = dot_padded(lhs, rhs)
-                gacc[k, :, n:n + 512] = p if c == 0 else gacc[k, :, n:n + 512] + p
+                p = p if c == 0 else gacc[k, :, n:n + 512] + p
+                if last:
+                    both.append(jnp.where(inv2 > 0, p * inv2, 0.0))
+                else:
+                    gacc[k, :, n:n + 512] = p
+            if last:
+                ubuf[:T, n:n + 512] = (both[0] * jax.nn.sigmoid(both[0]) * both[1]).astype(BF16)
 
     for c in range(NCH):
         phase(f'hop2_{c}')
@@ -379,13 +397,6 @@
     for c in range(NCH - GLAG, NCH):
         phase(f'hop3_{c}')
         gate_up(c)
-    phase('act')
-    inv2 = lax.rsqrt(jnp.sum(squares[0], axis=-1, keepdims=True) / D + NORM_EPS)
-    inv2 = inv2 * g_top
-    gate = jnp.where(inv2 > 0, gacc[0] * inv2, 0.0)
-    up = jnp.where(inv2 > 0, gacc[1] * inv2, 0.0)
-    ubuf[:T] = (gate * jax.nn.sigmoid(gate) * up).astype(BF16)
-
     phase('down')
     wait(ld_wd)
     mine = rows_of(chip)

time: 32.9 us -> 32.7 us (level)
  no operation moved by 1% of the time
where the time goes in v5:
time: 32.7 us; the launch traced here: 32.6 us
  Pallas kernels  31.2 us (95%)
  between operations  1.32 us (4%)
    pallas_call x1, Pallas kernels, local_layer(): pl.pallas_call(layer_kernel, name='layer', out_shape=(jax.ShapeDtypeStruc...  29.1 us
    pallas_call x1, Pallas kernels, local_layer(): pl.pallas_call(cache_kernel, name='cache', out_shape=(jax.ShapeDtypeStruc...  2.14 us

profile of v5, /device:TPU:0, one launch (start us, length us, event | category | flops | bytes accessed | tf_op | source)
XLA Modules:
  0.0 32.6 jit_solution(15757673393758235892)
XLA Ops:
  1.3 0.0 copy-start
  1.3 0.0 copy-start.1
  1.3 29.1 %layer.1 = (bf16[8192,3072]{1,0:T(8,128)(2,1)}, bf16[196608,128]{1,0:T(8,128)(2,1)}, bf16[196608,128]{1,0:T(8,128)(2,1)}) custom-call(s32[1]{0:T(128)S(6)} %copy.17.start_hbm.start_ref, f32[1,128]{1,0:T(1,128)} %constant.2.clone.invf_hbm, bf16[16,3072]{1,0:T(8,128)(2,1)} %bitcast.24, bf16[24,128]{1,0:T(8,128)(2,1)} %bitcast.25, bf16[24,128]{1,0:T(8,128)(2,1)} %bitcast.26, ...), custom_call_target="tpu_custom_call" | custom-call | flops 3200000000 | bytes 80000000 | tf_op jit(solution)/shard_map/layer/pallas_call | solution.py:511
  30.4 0.0 copy-done
  30.4 0.0 copy-done.1
  30.4 2.1 %cache.1 = (bf16[16,512,128]{2,1,0:T(8,128)(2,1)}, bf16[16,512,128]{2,1,0:T(8,128)(2,1)}, bf16[16,3072]{1,0:T(8,128)(2,1)}) custom-call(s32[1]{0:T(128)S(6)} %copy.17.start_hbm.start_ref, bf16[16,512,128]{2,1,0:T(8,128)(2,1)S(1)} %bitcast.17, bf16[16,512,128]{2,1,0:T(8,128)(2,1)S(1)} %bitcast.19, bf16[196608,128]{1,0:T(8,128)(2,1)} %get-tuple-element.9.kch, ...), custom_call_target="tpu_custom_call" | custom-call | tf_op jit(solution)/shard_map/cache/pallas_call | solution.py:537
Async XLA Ops:
  1.3 29.1 %copy-start = (bf16[1,4096,2,128]{3,2,1,0:T(2,128)(2,1)S(1)}, bf16[1,4096,2,128]{3,2,1,0:T(2,128)(2,1)}, u32[]{:S(2)}) copy-start(bf16[1,4096,2,128]{3,2,1,0:T(2,128)(2,1)} %param.16) | copy-start | bytes 6291460
  1.3 29.1 %copy-start.1 = (bf16[1,4096,2,128]{3,2,1,0:T(2,128)(2,1)S(1)}, bf16[1,4096,2,128]{3,2,1,0:T(2,128)(2,1)}, u32[]{:S(2)}) copy-start(bf16[1,4096,2,128]{3,2,1,0:T(2,128)(2,1)} %param.17) | copy-start | bytes 6291460
